TPU v7x, 256 devices: a 8x8x2 block of a 8x8x16 slice. The times are simulated.
256 devices in a mesh: groups: 2 (over z), dev: 16 (over y, core), tp: 8 (over x).
Axes of the slice: x: 8, y: 8, z: 2, core: 2. Of those that a mesh axis runs over, the one named last changes fastest.
The devices are a block of a 8x8x16 slice.
Arguments:
- hidden_states: bfloat16 [20480, 5120], P(('groups', 'dev'), 'tp'), parts along dimension 0, may hold values from -6 to 6
- norm_gain: bfloat16 [5120], replicated, may hold values from 0.25 to 1.75
- w_query: bfloat16 [5120, 5120], P('dev', 'tp'), may hold values from -2 to 2
- w_key: bfloat16 [5120, 1024], P('dev', 'tp'), may hold values from -2 to 2
- w_value: bfloat16 [5120, 1024], P('dev', 'tp'), may hold values from -0.078125 to 0.078125
- prompt_blocks: int32 [16], P('groups'), parts along dimension 0, may hold values from 1 to 11, 80 in all
- owner_map: int32 [160], P(('groups', 'dev')), parts along dimension 0, may hold values from 0 to 15, as said below
- slot_table: int32 [32, 32], P(('groups', 'dev')), parts along dimension 0, may hold values from 0 to 31, each once within a row
Outputs:
- context: bfloat16 [20480, 5120], P(('groups', 'dev'), 'tp'), parts along dimension 0
- kv_cache: bfloat16 [1024, 128, 2048], P(('groups', 'dev'), None, 'tp'), parts along dimension 0
There are 2 independent parts, one for each index of `groups`. A program takes and returns all parts, laid end to end along the dimension named above; an argument that names none is the same for every part. Nothing has to cross between parts.
Inputs may be any that keep to these rules, and one draw needn't show every extreme that they name: `prompt_blocks`: the entries sum to 80. `owner_map`: each device's 5 blocks name any owner at most 2 times, and no owner receives more than 32 blocks; in every draw some owner receives 2 blocks from every device. `slot_table`: each row is a permutation of 0 to 31.
All inputs are finite; a program needn't handle non-finite values.
Results may differ from a plain program's by a relative error of at most 0.0079.
Values may be sent and summed in bfloat16 or wider, within the bound.
No kernel may reach another device: no remote copies, remote signals or barrier semaphores. Data moves between devices by JAX's collectives and lax.ppermute only.
A program may use at most 128 MiB of HBM per device.

v0:
```python
import functools
import math

import jax
import jax.numpy as jnp
from jax import lax
from jax.experimental import pallas as pl
from jax.experimental.pallas import tpu as pltpu
from jax.sharding import PartitionSpec as P


HD = 128
BLOCK = 128
LEN_BLOCKS = 11
EPSILON = 1e-06
THETA = 1000000.0
VMEM = pltpu.MemorySpace.VMEM
SMEM = pltpu.MemorySpace.SMEM
VMEM_ALL = 60 * 1024 * 1024
VMEM_SOME = 24 * 1024 * 1024


def ring(block, axis, hop, last_ahead):
    size = lax.axis_size(axis)
    count = size // hop
    ahead = [(i, (i + hop) % size) for i in range(size)]
    back = [(i, (i - hop) % size) for i in range(size)]
    got = {0: block}
    up = down = block
    for step in range(1, count // 2):
        up = lax.ppermute(up, axis, ahead)
        down = lax.ppermute(down, axis, back)
        got[count - step] = up
        got[step] = down
    if last_ahead:
        got[count // 2] = lax.ppermute(up, axis, ahead)
    else:
        got[count // 2] = lax.ppermute(down, axis, back)
    return [got[i] for i in range(count)]


def swap(block, axis):
    size = lax.axis_size(axis)
    return lax.ppermute(block, axis, [(i, i ^ 1) for i in range(size)])


def proj_kernel(place, *refs, count, rows, feat, width, lo, n_q, kv, has_scale, has_old):
    x_refs = refs[:count]
    mine, other, gain, cos, sin = refs[count : count + 5]
    at = count + 5
    old = scale_in = None
    if has_old:
        old = refs[at]
        at += 1
    if has_scale:
        scale_in = refs[at]
        at += 1
    n_out = (1 if n_q else 0) + (1 if kv else 0) + (0 if has_scale else 1)
    outs = refs[at : at + n_out]
    xbuf, wbuf, acc, scale_ref, sem_x, sem_w = refs[at + n_out :]
    tp, chip, core = place[0], place[1], place[2]
    w_rows = feat // 2
    tile = 64

    def x_copy(i, src):
        spot = pl.multiple_of(i * feat, 128)
        return pltpu.make_async_copy(src, xbuf.at[:, pl.ds(spot, feat)], sem_x.at[i])

    def w_copy(i, which):
        src = mine if which == 0 else other
        spot = core if which == 0 else 1 - core
        rel = jnp.bitwise_and(tp + i - chip, count - 1)
        return pltpu.make_async_copy(
            src.at[rel, pl.ds(0, w_rows), pl.ds(lo, width)],
            wbuf.at[pl.ds(pl.multiple_of(i * feat + spot * w_rows, 64), w_rows)],
            sem_w.at[2 * i + which],
        )

    for i in range(count):
        x_copy(i, x_refs[i]).start()

    def fetch(i, unused):
        w_copy(i, 0).start()
        w_copy(i, 1).start()
        return unused

    lax.fori_loop(0, count, fetch, 0)
    acc[...] = jnp.zeros_like(acc)
    if has_scale:
        scale_ref[...] = scale_in[...]
    else:
        scale_ref[...] = jnp.zeros_like(scale_ref)

        def add_piece(i, unused):
            x_copy(i, x_refs[0]).wait()

            def add_squares(r, unused):
                at_rows = pl.ds(pl.multiple_of(r * tile, tile), tile)
                total = scale_ref[at_rows]
                for g in range(feat // 128):
                    at_col = pl.ds(pl.multiple_of(i * feat + g * 128, 128), 128)
                    part = xbuf[at_rows, at_col].astype(jnp.float32)
                    total = total + part * part
                scale_ref[at_rows] = total
                return unused

            return lax.fori_loop(0, rows // tile, add_squares, unused)

        lax.fori_loop(0, count, add_piece, 0)
        mean = jnp.sum(scale_ref[...], axis=1, keepdims=True) * (1.0 / (feat * count))
        scale_ref[...] = jnp.broadcast_to(lax.rsqrt(mean + EPSILON), scale_ref.shape)
        outs[-1][...] = scale_ref[...]

    def multiply(c, unused):
        for k in range(2):
            i = 2 * c + k
            feature = jnp.bitwise_and(tp + i, count - 1)
            if has_scale:
                x_copy(i, x_refs[0]).wait()

            def normalize(r, unused):
                at_rows = pl.ds(pl.multiple_of(r * tile, tile), tile)
                scale = scale_ref[at_rows]
                for g in range(feat // 128):
                    at_col = pl.ds(pl.multiple_of(i * feat + g * 128, 128), 128)
                    part = xbuf[at_rows, at_col].astype(jnp.float32)
                    by = gain[feature, :, g * 128 : (g + 1) * 128]
                    xbuf[at_rows, at_col] = (part * scale * by).astype(jnp.bfloat16)
                return unused

            lax.fori_loop(0, rows // tile, normalize, 0)
            w_copy(i, 0).wait()
            w_copy(i, 1).wait()
        span = pl.ds(pl.multiple_of(c * 2 * feat, 256), 2 * feat)
        acc[...] += jnp.dot(xbuf[:, span], wbuf[span], preferred_element_type=jnp.float32)
        return unused

    lax.fori_loop(0, count // 2, multiply, 0)
    cosine = cos[...]
    sine = sin[...]

    def rotated(at_col):
        head = acc[:, at_col : at_col + HD]
        return (head * cosine + pltpu.roll(head, HD // 2, 1) * sine).astype(jnp.bfloat16)

    for h in range(n_q):
        outs[0][h] = rotated(h * HD)
    if kv:
        out = outs[1 if n_q else 0]
        base = 0
        if has_old:
            base = old.shape[0]
            out[:base] = old[...]
        k_at = n_q * HD
        out[base : base + rows, :HD] = rotated(k_at)
        out[base : base + rows, HD:] = acc[:, k_at + HD : k_at + 2 * HD].astype(jnp.bfloat16)


def project(place, pieces, mine, other, gain, cos, sin, n_q, kv, lo, old=None, scale=None):
    count = len(pieces)
    rows, feat = pieces[0].shape
    width = n_q * HD + (2 * HD if kv else 0)
    outs = []
    if n_q:
        outs.append(jax.ShapeDtypeStruct((n_q, rows, HD), jnp.bfloat16))
    if kv:
        extra = old.shape[0] if old is not None else 0
        outs.append(jax.ShapeDtypeStruct((rows + extra, 2 * HD), jnp.bfloat16))
    if scale is None:
        outs.append(jax.ShapeDtypeStruct((rows, 128), jnp.float32))
    kernel = functools.partial(
        proj_kernel,
        count=count,
        rows=rows,
        feat=feat,
        width=width,
        lo=lo,
        n_q=n_q,
        kv=kv,
        has_scale=scale is not None,
        has_old=old is not None,
    )
    operands = [place, *pieces, mine, other, gain, cos, sin]
    specs = [pl.BlockSpec(memory_space=SMEM)]
    specs += [pl.BlockSpec(memory_space=pl.ANY)] * (count + 2)
    specs += [pl.BlockSpec(memory_space=VMEM)] * 3
    for more in (old, scale):
        if more is not None:
            operands.append(more)
            specs.append(pl.BlockSpec(memory_space=VMEM))
    return pl.pallas_call(
        kernel,
        out_shape=tuple(outs),
        in_specs=specs,
        out_specs=tuple(pl.BlockSpec(memory_space=VMEM) for _ in outs),
        scratch_shapes=[
            pltpu.VMEM((rows, count * feat), jnp.bfloat16),
            pltpu.VMEM((count * feat, width), jnp.bfloat16),
            pltpu.VMEM((rows, width), jnp.float32),
            pltpu.VMEM((rows, 128), jnp.float32),
            pltpu.SemaphoreType.DMA((count,)),
            pltpu.SemaphoreType.DMA((2 * count,)),
        ],
        compiler_params=pltpu.CompilerParams(vmem_limit_bytes=VMEM_ALL),
        cost_estimate=pl.CostEstimate(
            flops=2 * rows * feat * count * width,
            bytes_accessed=2 * feat * count * (width + rows),
            transcendentals=0,
        ),
    )(*operands)


def attend_kernel(
    info, q_a, q_b, far, near, own, *refs, lo, hi
):
    out, qbuf, kvbuf, sbuf, mbuf, lbuf, obuf, tbuf, sems, sem_out = refs[-10:]
    heads, part, _ = q_a.shape
    tok = own.shape[0]
    local = tok // BLOCK
    back = 2 * local
    copies = [
        pltpu.make_async_copy(q_a, qbuf.at[:, pl.ds(0, part)], sems.at[0]),
        pltpu.make_async_copy(q_b, qbuf.at[:, pl.ds(part, tok - part)], sems.at[1]),
        pltpu.make_async_copy(far, kvbuf.at[pl.ds(BLOCK, tok)], sems.at[2]),
        pltpu.make_async_copy(near, kvbuf.at[pl.ds(BLOCK + tok, tok)], sems.at[3]),
        pltpu.make_async_copy(own, kvbuf.at[pl.ds(BLOCK + 2 * tok, tok)], sems.at[4]),
    ]
    for copy in copies:
        copy.start()
    kvbuf[:BLOCK] = jnp.zeros((BLOCK, 2 * HD), jnp.bfloat16)
    for copy in copies:
        copy.wait()
    first = info[0]
    n_prompts = info.shape[0] - 1
    factor = math.log2(math.e) / math.sqrt(HD)
    rows = heads * BLOCK
    row = lax.broadcasted_iota(jnp.int32, (BLOCK, BLOCK), 0)
    col = lax.broadcasted_iota(jnp.int32, (BLOCK, BLOCK), 1)
    causal = col <= row

    def result_copy(i):
        at = pl.ds(pl.multiple_of(i * BLOCK, BLOCK), BLOCK)
        return pltpu.make_async_copy(tbuf.at[i - lo], out.at[at], sem_out.at[i - lo])

    def one_block(i, unused):
        block = first + i

        def find(p, state):
            start, best = state
            best = jnp.where(start <= block, start, best)
            return start + info[1 + p], best

        _, begin = lax.fori_loop(0, n_prompts, find, (jnp.int32(0), jnp.int32(0)))
        low = jnp.maximum(begin - first + back, i) + 1
        last = back + i + 1
        pairs = (last - low + 2) // 2
        q = qbuf[:, pl.ds(pl.multiple_of(i * BLOCK, BLOCK), BLOCK), :].reshape(rows, HD)

        def span(t):
            return pl.ds(pl.multiple_of((last - 1 - 2 * t) * BLOCK, BLOCK), 2 * BLOCK)

        def score(t, h):
            s = lax.dot_general(
                q[h * BLOCK : (h + 1) * BLOCK],
                kvbuf[span(t), :HD],
                (((1,), (1,)), ((), ())),
                preferred_element_type=jnp.float32,
            )
            inside = last - 1 - 2 * t >= low
            bias = jnp.where(inside, 0.0, -1e30)
            return s[:, :BLOCK] * factor + bias, s[:, BLOCK:] * factor

        for h in range(heads):
            at = slice(h * BLOCK, (h + 1) * BLOCK)
            left, right = score(0, h)
            right = jnp.where(causal, right, -1e30)
            sbuf[0, at, :BLOCK] = left
            sbuf[0, at, BLOCK:] = right
            mbuf[at] = jnp.maximum(left, right)

        def upward(t, unused):
            for h in range(heads):
                at = slice(h * BLOCK, (h + 1) * BLOCK)
                left, right = score(t, h)
                sbuf[t, at, :BLOCK] = left
                sbuf[t, at, BLOCK:] = right
                mbuf[at] = jnp.maximum(mbuf[at], jnp.maximum(left, right))
            return unused

        lax.fori_loop(1, pairs, upward, 0)
        top = jnp.max(mbuf[...], axis=1, keepdims=True)
        mbuf[...] = jnp.broadcast_to(top, mbuf.shape)
        lbuf[...] = jnp.zeros_like(lbuf)
        obuf[...] = jnp.zeros_like(obuf)

        def gather(t, unused):
            for h in range(heads):
                at = slice(h * BLOCK, (h + 1) * BLOCK)
                peak = mbuf[at]
                left = jnp.exp2(sbuf[t, at, :BLOCK] - peak)
                right = jnp.exp2(sbuf[t, at, BLOCK:] - peak)
                lbuf[at] += left + right
                p = jnp.concatenate([left.astype(jnp.bfloat16), right.astype(jnp.bfloat16)], axis=1)
                obuf[at] += jnp.dot(p, kvbuf[span(t), HD:], preferred_element_type=jnp.float32)
            return unused

        lax.fori_loop(0, pairs, gather, 0)
        total = jnp.sum(lbuf[...], axis=1, keepdims=True)
        result = (obuf[...] / total).astype(jnp.bfloat16)
        for h in range(heads):
            tbuf[i - lo, :, h * HD : (h + 1) * HD] = result[h * BLOCK : (h + 1) * BLOCK]
        result_copy(i).start()
        return unused

    lax.fori_loop(lo, hi, one_block, 0)
    for i in range(lo, hi):
        result_copy(i).wait()


def attend(info, q_a, q_b, far, near, own, lo, hi, base=None):
    heads = q_a.shape[0]
    tok = own.shape[0]
    operands = [info, q_a, q_b, far, near, own]
    if base is not None:
        operands.append(base)
    return pl.pallas_call(
        functools.partial(attend_kernel, lo=lo, hi=hi),
        out_shape=jax.ShapeDtypeStruct((tok, heads * HD), jnp.bfloat16),
        in_specs=[pl.BlockSpec(memory_space=SMEM)]
        + [pl.BlockSpec(memory_space=pl.ANY)] * (len(operands) - 1),
        out_specs=pl.BlockSpec(memory_space=pl.ANY),
        scratch_shapes=[
            pltpu.VMEM((heads, tok, HD), jnp.bfloat16),
            pltpu.VMEM((3 * tok + BLOCK, 2 * HD), jnp.bfloat16),
            pltpu.VMEM(((LEN_BLOCKS + 1) // 2, heads * BLOCK, 2 * BLOCK), jnp.float32),
            pltpu.VMEM((heads * BLOCK, BLOCK), jnp.float32),
            pltpu.VMEM((heads * BLOCK, BLOCK), jnp.float32),
            pltpu.VMEM((heads * BLOCK, HD), jnp.float32),
            pltpu.VMEM((hi - lo, BLOCK, heads * HD), jnp.bfloat16),
            pltpu.SemaphoreType.DMA((5,)),
            pltpu.SemaphoreType.DMA((hi - lo,)),
        ],
        input_output_aliases={6: 0} if base is not None else {},
        compiler_params=pltpu.CompilerParams(vmem_limit_bytes=VMEM_SOME),
        cost_estimate=pl.CostEstimate(
            flops=2 * 10**9 * (hi - lo), bytes_accessed=4 * 10**6, transcendentals=10**6
        ),
    )(*operands)


def cache_kernel(place, own_mine, own_other, table, mine, other, mine_mid, other_mid, out, sem, *, local, count, tok):
    chip, core, me = place[1], place[2], place[3]
    mid = count // 2
    slots = out.shape[0]

    def put(src, at_row, slot):
        return pltpu.make_async_copy(src.at[pl.ds(pl.multiple_of(at_row, BLOCK), BLOCK)], out.at[slot], sem)

    def one(source, rank):
        rel = jnp.bitwise_and(jnp.right_shift(source, 1) - chip, count - 1)
        same = jnp.bitwise_and(source, 1) == core
        middle = rel == mid
        spot = jnp.where(rel > mid, rel - 1, jnp.where(middle, 0, rel))
        for inner in range(local):
            entry = rel * local + inner
            hit = jnp.where(same, own_mine[entry], own_other[entry]) == me

            @pl.when(hit)
            def _():
                slot = table[0, rank]
                at_row = spot * tok + inner * BLOCK

                @pl.when(same & jnp.logical_not(middle))
                def _():
                    put(mine, at_row, slot).start()

                @pl.when(jnp.logical_not(same) & jnp.logical_not(middle))
                def _():
                    put(other, at_row, slot).start()

                @pl.when(same & middle)
                def _():
                    put(mine_mid, at_row, slot).start()

                @pl.when(jnp.logical_not(same) & middle)
                def _():
                    put(other_mid, at_row, slot).start()

            rank = rank + hit.astype(jnp.int32)
        return rank

    found = lax.fori_loop(0, 2 * count, one, jnp.int32(0))

    def clear(r, unused):
        out[table[0, r]] = jnp.zeros(out.shape[1:], out.dtype)
        return unused

    lax.fori_loop(found, slots, clear, 0)

    def settle(r, unused):
        put(mine, 0, 0).wait()
        return unused

    lax.fori_loop(0, found, settle, 0)


def fill_cache(place, own_mine, own_other, table, mine, other, mine_mid, other_mid, local, count):
    tok = mine_mid.shape[0]
    slots = table.shape[1]
    return pl.pallas_call(
        functools.partial(cache_kernel, local=local, count=count, tok=tok),
        out_shape=jax.ShapeDtypeStruct((slots, BLOCK, mine.shape[1]), jnp.bfloat16),
        in_specs=[pl.BlockSpec(memory_space=SMEM)] * 4 + [pl.BlockSpec(memory_space=pl.ANY)] * 4,
        out_specs=pl.BlockSpec(memory_space=VMEM),
        scratch_shapes=[pltpu.SemaphoreType.DMA],
        compiler_params=pltpu.CompilerParams(vmem_limit_bytes=VMEM_SOME),
    )(place, own_mine, own_other, table, mine, other, mine_mid, other_mid)


def on_device(
    hidden_states, norm_gain, w_query, w_key, w_value, prompt_blocks, owner_map, slot_table
):
    tok, feat = hidden_states.shape
    n_dev = lax.axis_size("dev")
    n_tp = lax.axis_size("tp")
    device = lax.axis_index("dev")
    count = n_dev // 2
    assert count & (count - 1) == 0 and count == n_tp
    mid = count // 2
    local = tok // BLOCK
    heads = w_query.shape[1] // HD
    place = jnp.stack([lax.axis_index("tp"), device // 2, device % 2, device]).astype(jnp.int32)

    part = tok // 2
    x_a = ring(hidden_states[:part], "tp", 1, True)
    x_b = ring(hidden_states[part:], "tp", 1, False)

    weights = jnp.concatenate([w_query, w_key, w_value], axis=1)
    w_rows, w_cols = weights.shape
    labels = jnp.pad(owner_map.astype(jnp.bfloat16)[None], ((0, 7), (0, w_cols - local)))
    weights = jnp.concatenate([weights, labels], axis=0)
    mine = jnp.stack(ring(weights, "dev", 2, True))
    other = swap(mine, "dev")
    own_mine = mine[:, w_rows, :local].astype(jnp.int32).reshape(-1)
    own_other = other[:, w_rows, :local].astype(jnp.int32).reshape(-1)
    place, own_mine, own_other = lax.optimization_barrier((place, own_mine, own_other))

    token_rows = device * tok + jnp.arange(tok, dtype=jnp.int32)
    starts = (jnp.cumsum(prompt_blocks) - prompt_blocks) * BLOCK
    start_of = jnp.max(jnp.where(token_rows[:, None] >= starts[None, :], starts[None, :], 0), axis=1)
    offsets = token_rows - start_of
    freq_index = jnp.arange(HD // 2, dtype=jnp.float32)
    inverse = jnp.exp(freq_index * (-2.0 * math.log(THETA) / HD))
    angles = offsets.astype(jnp.float32)[:, None] * inverse[None, :]
    cosine, sine = jnp.cos(angles), jnp.sin(angles)
    cos = jnp.concatenate([cosine, cosine], axis=1)
    sin = jnp.concatenate([-sine, sine], axis=1)
    gain = norm_gain.astype(jnp.float32).reshape(n_tp, 1, feat)

    q_width = heads * HD
    q_a, kv_a, _ = project(place, x_a, mine, other, gain, cos[:part], sin[:part], heads, True, 0)
    kv, scale_b = project(
        place, x_b, mine, other, gain, cos[part:], sin[part:], 0, True, q_width, old=kv_a
    )
    (q_b,) = project(
        place, x_b, mine, other, gain, cos[part:], sin[part:], heads, False, 0, scale=scale_b
    )

    near = lax.ppermute(kv, "dev", [(i, i + 1) for i in range(n_dev - 1)])
    k_got = ring(kv, "dev", 2, False)
    far = k_got[count - 1]
    info = jnp.concatenate([(device * local)[None].astype(jnp.int32), prompt_blocks])
    cuts = (0, local // 2, local - 1, local)
    context = attend(info, q_a, q_b, far, near, kv, cuts[0], cuts[1])
    context = attend(info, q_a, q_b, far, near, kv, cuts[1], cuts[2], base=context)
    context = attend(info, q_a, q_b, far, near, kv, cuts[2], cuts[3], base=context)
    k_mine = jnp.concatenate([k_got[i] for i in range(count) if i != mid], axis=0)
    k_other = swap(k_mine, "dev")
    k_mid_other = swap(k_got[mid], "dev")
    kv_cache = fill_cache(
        place, own_mine, own_other, slot_table, k_mine, k_other, k_got[mid], k_mid_other, local, count
    )
    return (context, kv_cache)


def solution(mesh):
    in_specs = (
        P(("groups", "dev"), "tp"),
        P(),
        P("dev", "tp"),
        P("dev", "tp"),
        P("dev", "tp"),
        P("groups"),
        P(("groups", "dev")),
        P(("groups", "dev"), None),
    )
    out_specs = (P(("groups", "dev"), "tp"), P(("groups", "dev"), None, "tp"))

    return jax.shard_map(on_device, mesh=mesh, in_specs=in_specs, out_specs=out_specs, check_vma=False)
```

profile of v0, /device:TPU:513, one launch (start us, length us, event | category | flops | bytes accessed | tf_op | source)
XLA Modules:
  0.0 228.3 jit_solution(8560270243374718648)
XLA Ops:
  1.3 1.1 fusion.1
  2.4 3.4 %collective-permute-start.3 = (bf16[328,896]{1,0:T(8,128)(2,1)S(1)}, bf16[328,896]{1,0:T(8,128)(2,1)S(1)}, u32[]{:S(2)}, u32[]{:S(2)}) collective-permute-start(bf16[328,896]{1,0:T(8,128)(2,1)S(1)} %fusion.1), channel_id=1, source_target_pairs={{0,16},{8,24},{16,32},{24,40},{32,48},{40,56},{48,64},{56,72},{64,... | collective-permute-start | bytes 1763336 | tf_op jit(solution)/shard_map/ppermute | solution.py:31
  5.9 9.2 %collective-permute-start = (bf16[328,896]{1,0:T(8,128)(2,1)S(1)}, bf16[328,896]{1,0:T(8,128)(2,1)S(1)}, u32[]{:S(2)}, u32[]{:S(2)}) collective-permute-start(bf16[328,896]{1,0:T(8,128)(2,1)S(1)} %fusion.1), channel_id=1, source_target_pairs={{0,112},{8,120},{16,0},{24,8},{32,16},{40,24},{48,32},{56,40},{64,... | collective-permute-start | bytes 1763336 | tf_op jit(solution)/shard_map/ppermute | solution.py:32
  15.1 7.1 %collective-permute-done.3 = bf16[328,896]{1,0:T(8,128)(2,1)S(1)} collective-permute-done((bf16[328,896]{1,0:T(8,128)(2,1)S(1)}, bf16[328,896]{1,0:T(8,128)(2,1)S(1)}, u32[]{:S(2)}, u32[]{:S(2)}) %collective-permute-start.3) | collective-permute-done | bytes 587808 | tf_op jit(solution)/shard_map/ppermute | solution.py:31
  22.2 7.0 %collective-permute-start.1 = (bf16[328,896]{1,0:T(8,128)(2,1)S(1)}, bf16[328,896]{1,0:T(8,128)(2,1)S(1)}, u32[]{:S(2)}, u32[]{:S(2)}) collective-permute-start(bf16[328,896]{1,0:T(8,128)(2,1)S(1)} %collective-permute-done), channel_id=1, source_target_pairs={{0,112},{8,120},{16,0},{24,8},{32,16},{40,24},{48,32},{56,40},{64,... | collective-permute-start | bytes 1763336 | tf_op jit(solution)/shard_map/ppermute | solution.py:32
  29.2 10.4 %collective-permute-done.4 = bf16[328,896]{1,0:T(8,128)(2,1)S(1)} collective-permute-done((bf16[328,896]{1,0:T(8,128)(2,1)S(1)}, bf16[328,896]{1,0:T(8,128)(2,1)S(1)}, u32[]{:S(2)}, u32[]{:S(2)}) %collective-permute-start.4) | collective-permute-done | bytes 587808 | tf_op jit(solution)/shard_map/ppermute | solution.py:31
  39.6 3.0 %collective-permute-start.2 = (bf16[328,896]{1,0:T(8,128)(2,1)S(1)}, bf16[328,896]{1,0:T(8,128)(2,1)S(1)}, u32[]{:S(2)}, u32[]{:S(2)}) collective-permute-start(bf16[328,896]{1,0:T(8,128)(2,1)S(1)} %collective-permute-done.1), channel_id=1, source_target_pairs={{0,112},{8,120},{16,0},{24,8},{32,16},{40,24},{48,32},{56,40},{64,... | collective-permute-start | bytes 1763336 | tf_op jit(solution)/shard_map/ppermute | solution.py:32
  42.6 2.0 bitcast_dynamic-update-slice_fusion.7
  44.6 9.3 %collective-permute-done.5 = bf16[328,896]{1,0:T(8,128)(2,1)S(1)} collective-permute-done((bf16[328,896]{1,0:T(8,128)(2,1)S(1)}, bf16[328,896]{1,0:T(8,128)(2,1)S(1)}, u32[]{:S(2)}, u32[]{:S(2)}) %collective-permute-start.5) | collective-permute-done | bytes 587808 | tf_op jit(solution)/shard_map/ppermute | solution.py:31
  53.9 0.9 bitcast_dynamic-update-slice_fusion.6
  56.6 12.8 %collective-permute-done.6 = bf16[328,896]{1,0:T(8,128)(2,1)S(1)} collective-permute-done((bf16[328,896]{1,0:T(8,128)(2,1)S(1)}, bf16[328,896]{1,0:T(8,128)(2,1)S(1)}, u32[]{:S(2)}, u32[]{:S(2)}) %collective-permute-start.6) | collective-permute-done | bytes 587808 | tf_op jit(solution)/shard_map/ppermute | solution.py:36
  71.1 0.9 bitcast_dynamic-update-slice_fusion.1
  72.8 11.0 %collective-permute-start.7 = (bf16[8,328,896]{2,1,0:T(8,128)(2,1)}, bf16[8,328,896]{2,1,0:T(8,128)(2,1)}, u32[]{:S(2)}, u32[]{:S(2)}) collective-permute-start(bf16[8,328,896]{2,1,0:T(8,128)(2,1)} %bitcast_dynamic-update-slice_fusion.refs_8_), channel_id=1, source_target_pairs={{0,8},{8,0},{16,24},{24,16},{32,40},{40,32},{48,56},{56,48},{64,72... | collective-permute-start | bytes 14106632 | tf_op jit(solution)/shard_map/ppermute | solution.py:44
  84.0 2.6 %collective-permute-start.15 = (bf16[320,640]{1,0:T(8,128)(2,1)S(1)}, bf16[320,640]{1,0:T(8,128)(2,1)S(1)}, u32[]{:S(2)}, u32[]{:S(2)}) collective-permute-start(bf16[320,640]{1,0:T(8,128)(2,1)S(1)} %get-tuple-element.16.refs_0_), channel_id=1, source_target_pairs={{0,7},{1,0},{2,1},{3,2},{4,3},{5,4},{6,5},{7,6},{8,15},{9,8},{10,9... | collective-permute-start | bytes 1228808 | tf_op jit(solution)/shard_map/ppermute | solution.py:32
  86.7 1.4 collective-permute-start.19
  88.3 7.9 %collective-permute-done.11.refs_7_ = bf16[320,640]{1,0:T(8,128)(2,1)S(1)} collective-permute-done((bf16[320,640]{1,0:T(8,128)(2,1)S(1)}, bf16[320,640]{1,0:T(8,128)(2,1)S(1)}, u32[]{:S(2)}, u32[]{:S(2)}) %collective-permute-start.11) | collective-permute-done | bytes 409632 | tf_op jit(solution)/shard_map/ppermute | solution.py:31
  96.3 2.8 %collective-permute-start.16 = (bf16[320,640]{1,0:T(8,128)(2,1)S(1)}, bf16[320,640]{1,0:T(8,128)(2,1)S(1)}, u32[]{:S(2)}, u32[]{:S(2)}) collective-permute-start(bf16[320,640]{1,0:T(8,128)(2,1)S(1)} %collective-permute-done.15.refs_1_), channel_id=1, source_target_pairs={{0,7},{1,0},{2,1},{3,2},{4,3},{5,4},{6,5},{7,6},{8,15},{9,8},{10,9... | collective-permute-start | bytes 1228808 | tf_op jit(solution)/shard_map/ppermute | solution.py:32
  99.1 4.9 %collective-permute-done.8.refs_1_ = bf16[320,640]{1,0:T(8,128)(2,1)S(1)} collective-permute-done((bf16[320,640]{1,0:T(8,128)(2,1)S(1)}, bf16[320,640]{1,0:T(8,128)(2,1)S(1)}, u32[]{:S(2)}, u32[]{:S(2)}) %collective-permute-start.8) | collective-permute-done | bytes 409632 | tf_op jit(solution)/shard_map/ppermute | solution.py:32
  104.0 3.4 %collective-permute-start.9 = (bf16[320,640]{1,0:T(8,128)(2,1)S(1)}, bf16[320,640]{1,0:T(8,128)(2,1)}, u32[]{:S(2)}, u32[]{:S(2)}) collective-permute-start(bf16[320,640]{1,0:T(8,128)(2,1)S(1)} %collective-permute-done.8.refs_1_), channel_id=1, source_target_pairs={{0,7},{1,0},{2,1},{3,2},{4,3},{5,4},{6,5},{7,6},{8,15},{9,8},{10,9... | collective-permute-start | bytes 1228808 | tf_op jit(solution)/shard_map/ppermute | solution.py:32
  107.4 6.5 %collective-permute-done.12.refs_6_ = bf16[320,640]{1,0:T(8,128)(2,1)} collective-permute-done((bf16[320,640]{1,0:T(8,128)(2,1)S(1)}, bf16[320,640]{1,0:T(8,128)(2,1)}, u32[]{:S(2)}, u32[]{:S(2)}) %collective-permute-start.12) | collective-permute-done | bytes 409632 | tf_op jit(solution)/shard_map/ppermute | solution.py:31
  114.1 2.8 %collective-permute-start.17 = (bf16[320,640]{1,0:T(8,128)(2,1)S(1)}, bf16[320,640]{1,0:T(8,128)(2,1)S(1)}, u32[]{:S(2)}, u32[]{:S(2)}) collective-permute-start(bf16[320,640]{1,0:T(8,128)(2,1)S(1)} %collective-permute-done.16.refs_2_), channel_id=1, source_target_pairs={{0,7},{1,0},{2,1},{3,2},{4,3},{5,4},{6,5},{7,6},{8,15},{9,8},{10,9... | collective-permute-start | bytes 1228808 | tf_op jit(solution)/shard_map/ppermute | solution.py:32
  116.9 1.2 multiply_sine_fusion
  118.1 3.5 %collective-permute-done.9.refs_2_ = bf16[320,640]{1,0:T(8,128)(2,1)} collective-permute-done((bf16[320,640]{1,0:T(8,128)(2,1)S(1)}, bf16[320,640]{1,0:T(8,128)(2,1)}, u32[]{:S(2)}, u32[]{:S(2)}) %collective-permute-start.9) | collective-permute-done | bytes 409632 | tf_op jit(solution)/shard_map/ppermute | solution.py:32
  121.6 3.5 %collective-permute-start.10 = (bf16[320,640]{1,0:T(8,128)(2,1)}, bf16[320,640]{1,0:T(8,128)(2,1)}, u32[]{:S(2)}, u32[]{:S(2)}) collective-permute-start(bf16[320,640]{1,0:T(8,128)(2,1)} %collective-permute-done.9.refs_2_), channel_id=1, source_target_pairs={{0,7},{1,0},{2,1},{3,2},{4,3},{5,4},{6,5},{7,6},{8,15},{9,8},{10,9... | collective-permute-start | bytes 1228808 | tf_op jit(solution)/shard_map/ppermute | solution.py:32
  126.8 1.1 pad_maximum_fusion
  127.9 6.4 %collective-permute-done.20.refs_6_ = bf16[320,640]{1,0:T(8,128)(2,1)S(1)} collective-permute-done((bf16[320,640]{1,0:T(8,128)(2,1)S(1)}, bf16[320,640]{1,0:T(8,128)(2,1)S(1)}, u32[]{:S(2)}, u32[]{:S(2)}) %collective-permute-start.20) | collective-permute-done | bytes 409632 | tf_op jit(solution)/shard_map/ppermute | solution.py:31
  134.3 2.7 %collective-permute-start.18 = (bf16[320,640]{1,0:T(8,128)(2,1)S(1)}, bf16[320,640]{1,0:T(8,128)(2,1)}, u32[]{:S(2)}, u32[]{:S(2)}) collective-permute-start(bf16[320,640]{1,0:T(8,128)(2,1)S(1)} %collective-permute-done.17.refs_3_), channel_id=1, source_target_pairs={{0,7},{1,0},{2,1},{3,2},{4,3},{5,4},{6,5},{7,6},{8,15},{9,8},{10,9... | collective-permute-start | bytes 1228808 | tf_op jit(solution)/shard_map/ppermute | solution.py:38
  139.2 3.9 %collective-permute-done.14.refs_4_ = bf16[320,640]{1,0:T(8,128)(2,1)} collective-permute-done((bf16[320,640]{1,0:T(8,128)(2,1)}, bf16[320,640]{1,0:T(8,128)(2,1)}, u32[]{:S(2)}, u32[]{:S(2)}) %collective-permute-start.14) | collective-permute-done | bytes 409632 | tf_op jit(solution)/shard_map/ppermute | solution.py:36
  143.1 10.9 %shard_map.95 = (bf16[5,320,128]{2,1,0:T(8,128)(2,1)}, bf16[320,256]{1,0:T(8,128)(2,1)}, f32[320,128]{1,0:T(8,128)}) custom-call(s32[4]{0:T(128)} %pad_add_fusion.1.place, bf16[320,640]{1,0:T(8,128)(2,1)} %copy-done.6, bf16[320,640]{1,0:T(8,128)(2,1)} %copy-done.15, bf16[320,640]{1,0:T(8,128)(2,1)} %collective-permute-done.9.refs_2_, ...), custom_call_target="tpu_custom_call" | custom-call | flops 2936012800 | bytes 12451840 | tf_op jit(solution)/shard_map/pallas_call | solution.py:191
  154.9 8.1 %shard_map.96 = (bf16[640,256]{1,0:T(8,128)(2,1)}, f32[320,128]{1,0:T(8,128)}) custom-call(s32[4]{0:T(128)} %pad_add_fusion.1.place, bf16[320,640]{1,0:T(8,128)(2,1)} %copy-done.5, bf16[320,640]{1,0:T(8,128)(2,1)} %copy-done.7, bf16[320,640]{1,0:T(8,128)(2,1)} %copy-done.9, bf16[320,640]{1,0:T(8,128)(2,1)} %copy-done.11, ...), custom_call_target="tpu_custom_call" | custom-call | flops 838860800 | bytes 5898240 | tf_op jit(solution)/shard_map/pallas_call | solution.py:191
  163.1 1.4 collective-permute-start.22
  164.6 5.0 %collective-permute-done.24 = bf16[640,256]{1,0:T(8,128)(2,1)S(1)} collective-permute-done((bf16[640,256]{1,0:T(8,128)(2,1)}, bf16[640,256]{1,0:T(8,128)(2,1)S(1)}, u32[]{:S(2)}, u32[]{:S(2)}) %collective-permute-start.24) | collective-permute-done | bytes 327712 | tf_op jit(solution)/shard_map/ppermute | solution.py:32
  169.6 1.5 collective-permute-start.25
  171.1 5.2 %collective-permute-done.25 = bf16[640,256]{1,0:T(8,128)(2,1)S(1)} collective-permute-done((bf16[640,256]{1,0:T(8,128)(2,1)S(1)}, bf16[640,256]{1,0:T(8,128)(2,1)S(1)}, u32[]{:S(2)}, u32[]{:S(2)}) %collective-permute-start.25) | collective-permute-done | bytes 327712 | tf_op jit(solution)/shard_map/ppermute | solution.py:32
  176.3 1.9 collective-permute-start.26
  178.2 1.0 constant_dynamic-update-slice_fusion.6
  179.4 4.7 %collective-permute-done.26 = bf16[640,256]{1,0:T(8,128)(2,1)S(1)} collective-permute-done((bf16[640,256]{1,0:T(8,128)(2,1)S(1)}, bf16[640,256]{1,0:T(8,128)(2,1)S(1)}, u32[]{:S(2)}, u32[]{:S(2)}) %collective-permute-start.26) | collective-permute-done | bytes 327712 | tf_op jit(solution)/shard_map/ppermute | solution.py:32
  184.2 2.3 %collective-permute-done.28 = bf16[640,256]{1,0:T(8,128)(2,1)S(1)} collective-permute-done((bf16[640,256]{1,0:T(8,128)(2,1)S(1)}, bf16[640,256]{1,0:T(8,128)(2,1)S(1)}, u32[]{:S(2)}, u32[]{:S(2)}) %collective-permute-start.28) | collective-permute-done | bytes 327712 | tf_op jit(solution)/shard_map/ppermute | solution.py:31
  186.6 6.8 %collective-permute-start.29 = (bf16[4480,256]{1,0:T(8,128)(2,1)S(1)}, bf16[4480,256]{1,0:T(8,128)(2,1)}, u32[]{:S(2)}, u32[]{:S(2)}) collective-permute-start(bf16[4480,256]{1,0:T(8,128)(2,1)S(1)} %constant_dynamic-update-slice_fusion.mine), channel_id=1, source_target_pairs={{0,8},{8,0},{16,24},{24,16},{32,40},{40,32},{48,56},{56,48},{64,72... | collective-permute-start | bytes 6881288 | tf_op jit(solution)/shard_map/ppermute | solution.py:44
  193.3 1.9 collective-permute-start.23
  195.4 9.6 %shard_map.97.q_b = bf16[5,320,128]{2,1,0:T(8,128)(2,1)} custom-call(s32[4]{0:T(128)} %pad_add_fusion.1.place, bf16[320,640]{1,0:T(8,128)(2,1)} %copy-done.5, bf16[320,640]{1,0:T(8,128)(2,1)} %copy-done.7, bf16[320,640]{1,0:T(8,128)(2,1)} %copy-done.9, bf16[320,640]{1,0:T(8,128)(2,1)} %copy-done.11, bf16[320,640]{1,0:T(8,128)(2,1)} %collective-permute-done.18.refs_4_, ...), custom_call_target="tpu_custom_call" | custom-call | flops 2097152000 | bytes 9830400 | tf_op jit(solution)/shard_map/pallas_call | solution.py:191
  205.1 1.0 copy-done
  206.1 5.9 %shard_map.98.refs_0_ = bf16[640,640]{1,0:T(8,128)(2,1)} custom-call(s32[9]{0:T(128)S(1)} %pad_add_fusion.info, bf16[5,320,128]{2,1,0:T(8,128)(2,1)S(1)} %copy-done.4, bf16[5,320,128]{2,1,0:T(8,128)(2,1)S(1)} %copy-done, bf16[640,256]{1,0:T(8,128)(2,1)S(1)} %collective-permute-done.22.far, bf16[640,256]{1,0:T(8,128)(2,1)S(1)} %collective-permute-done.23.near, ...), custom_call_target="tpu_custom_call" | custom-call | flops 4000000000 | bytes 4000000 | tf_op jit(solution)/shard_map/pallas_call | solution.py:326
  212.0 2.0 collective-permute-done.30.mine_mid
  214.0 1.4 collective-permute-start.31
  215.4 6.9 %shard_map.99.refs_0_ = bf16[640,640]{1,0:T(8,128)(2,1)} custom-call(s32[9]{0:T(128)S(1)} %pad_add_fusion.info, bf16[5,320,128]{2,1,0:T(8,128)(2,1)S(1)} %copy-done.4, bf16[5,320,128]{2,1,0:T(8,128)(2,1)S(1)} %copy-done, bf16[640,256]{1,0:T(8,128)(2,1)S(1)} %collective-permute-done.22.far, ...), custom_call_target="tpu_custom_call", output_to_operand_aliasing={{}: (6, {})} | custom-call | flops 4000000000 | bytes 4000000 | tf_op jit(solution)/shard_map/pallas_call | solution.py:326
  222.3 2.5 %shard_map.100 = bf16[640,640]{1,0:T(8,128)(2,1)} custom-call(s32[9]{0:T(128)S(1)} %pad_add_fusion.info, bf16[5,320,128]{2,1,0:T(8,128)(2,1)S(1)} %copy-done.4, bf16[5,320,128]{2,1,0:T(8,128)(2,1)S(1)} %copy-done, bf16[640,256]{1,0:T(8,128)(2,1)S(1)} %collective-permute-done.22.far, ...), custom_call_target="tpu_custom_call", output_to_operand_aliasing={{}: (6, {})} | custom-call | flops 2000000000 | bytes 4000000 | tf_op jit(solution)/shard_map/pallas_call | solution.py:326
  224.9 3.2 %shard_map.101 = bf16[32,128,256]{2,1,0:T(8,128)(2,1)} custom-call(s32[4]{0:T(128)S(1)} %copy-done.2, s32[40]{0:T(128)S(1)} %reshape.63.own_mine, s32[40]{0:T(128)S(1)} %reshape.64.own_other, s32[1,32]{1,0:T(1,128)S(1)} %copy-done.3, bf16[4480,256]{1,0:T(8,128)(2,1)S(1)} %constant_dynamic-update-slice_fusion.mine, ...), custom_call_target="tpu_custom_call" | custom-call | tf_op jit(solution)/shard_map/pallas_call | solution.py:410
  (94 shorter events, 11.1 us)
Async XLA Ops:
  2.4 19.8 %collective-permute-start.3 = (bf16[328,896]{1,0:T(8,128)(2,1)S(1)}, bf16[328,896]{1,0:T(8,128)(2,1)S(1)}, u32[]{:S(2)}, u32[]{:S(2)}) collective-permute-start(bf16[328,896]{1,0:T(8,128)(2,1)S(1)} %fusion.1), channel_id=1, source_target_pairs={{0,16},{8,24},{16,32},{24,40},{32,48},{40,56},{48,64},{56,72},{64,... | collective-permute-start | bytes 1763336 | tf_op jit(solution)/shard_map/ppermute | solution.py:31
  5.9 16.4 %collective-permute-start = (bf16[328,896]{1,0:T(8,128)(2,1)S(1)}, bf16[328,896]{1,0:T(8,128)(2,1)S(1)}, u32[]{:S(2)}, u32[]{:S(2)}) collective-permute-start(bf16[328,896]{1,0:T(8,128)(2,1)S(1)} %fusion.1), channel_id=1, source_target_pairs={{0,112},{8,120},{16,0},{24,8},{32,16},{40,24},{48,32},{56,40},{64,... | collective-permute-start | bytes 1763336 | tf_op jit(solution)/shard_map/ppermute | solution.py:32
  22.2 17.4 %collective-permute-start.4 = (bf16[328,896]{1,0:T(8,128)(2,1)S(1)}, bf16[328,896]{1,0:T(8,128)(2,1)S(1)}, u32[]{:S(2)}, u32[]{:S(2)}) collective-permute-start(bf16[328,896]{1,0:T(8,128)(2,1)S(1)} %collective-permute-done.3), channel_id=1, source_target_pairs={{0,16},{8,24},{16,32},{24,40},{32,48},{40,56},{48,64},{56,72},{64,... | collective-permute-start | bytes 1763336 | tf_op jit(solution)/shard_map/ppermute | solution.py:31
  22.2 17.4 %collective-permute-start.1 = (bf16[328,896]{1,0:T(8,128)(2,1)S(1)}, bf16[328,896]{1,0:T(8,128)(2,1)S(1)}, u32[]{:S(2)}, u32[]{:S(2)}) collective-permute-start(bf16[328,896]{1,0:T(8,128)(2,1)S(1)} %collective-permute-done), channel_id=1, source_target_pairs={{0,112},{8,120},{16,0},{24,8},{32,16},{40,24},{48,32},{56,40},{64,... | collective-permute-start | bytes 1763336 | tf_op jit(solution)/shard_map/ppermute | solution.py:32
  39.6 14.3 %collective-permute-start.5 = (bf16[328,896]{1,0:T(8,128)(2,1)S(1)}, bf16[328,896]{1,0:T(8,128)(2,1)S(1)}, u32[]{:S(2)}, u32[]{:S(2)}) collective-permute-start(bf16[328,896]{1,0:T(8,128)(2,1)S(1)} %collective-permute-done.4), channel_id=1, source_target_pairs={{0,16},{8,24},{16,32},{24,40},{32,48},{40,56},{48,64},{56,72},{64,... | collective-permute-start | bytes 1763336 | tf_op jit(solution)/shard_map/ppermute | solution.py:31
  39.6 16.0 %collective-permute-start.2 = (bf16[328,896]{1,0:T(8,128)(2,1)S(1)}, bf16[328,896]{1,0:T(8,128)(2,1)S(1)}, u32[]{:S(2)}, u32[]{:S(2)}) collective-permute-start(bf16[328,896]{1,0:T(8,128)(2,1)S(1)} %collective-permute-done.1), channel_id=1, source_target_pairs={{0,112},{8,120},{16,0},{24,8},{32,16},{40,24},{48,32},{56,40},{64,... | collective-permute-start | bytes 1763336 | tf_op jit(solution)/shard_map/ppermute | solution.py:32
  53.9 15.4 %collective-permute-start.6 = (bf16[328,896]{1,0:T(8,128)(2,1)S(1)}, bf16[328,896]{1,0:T(8,128)(2,1)S(1)}, u32[]{:S(2)}, u32[]{:S(2)}) collective-permute-start(bf16[328,896]{1,0:T(8,128)(2,1)S(1)} %collective-permute-done.5), channel_id=1, source_target_pairs={{0,16},{8,24},{16,32},{24,40},{32,48},{40,56},{48,64},{56,72},{64,... | collective-permute-start | bytes 1763336 | tf_op jit(solution)/shard_map/ppermute | solution.py:36
  56.6 27.2 %copy-start.13 = (bf16[640,640]{1,0:T(8,128)(2,1)S(1)}, bf16[640,640]{1,0:T(8,128)(2,1)}, u32[]{:S(2)}) copy-start(bf16[640,640]{1,0:T(8,128)(2,1)} %param.8) | copy-start | bytes 2457604
  71.1 17.1 %copy-start.18 = (s32[8]{0:T(128)S(1)}, s32[8]{0:T(128)}, u32[]{:S(2)}) copy-start(s32[8]{0:T(128)} %param.13) | copy-start | bytes 100
  71.1 55.1 %copy-start.17 = (bf16[5120]{0:T(1024)(128)(2,1)S(1)}, bf16[5120]{0:T(1024)(128)(2,1)}, u32[]{:S(2)}) copy-start(bf16[5120]{0:T(1024)(128)(2,1)} %param.9) | copy-start | bytes 30724
  72.8 64.9 %collective-permute-start.7 = (bf16[8,328,896]{2,1,0:T(8,128)(2,1)}, bf16[8,328,896]{2,1,0:T(8,128)(2,1)}, u32[]{:S(2)}, u32[]{:S(2)}) collective-permute-start(bf16[8,328,896]{2,1,0:T(8,128)(2,1)} %bitcast_dynamic-update-slice_fusion.refs_8_), channel_id=1, source_target_pairs={{0,8},{8,0},{16,24},{24,16},{32,40},{40,32},{48,56},{56,48},{64,72... | collective-permute-start | bytes 14106632 | tf_op jit(solution)/shard_map/ppermute | solution.py:44
  83.9 59.3 %copy-start.6 = (bf16[320,640]{1,0:T(8,128)(2,1)}, bf16[320,640]{1,0:T(8,128)(2,1)S(1)}, u32[]{:S(2)}) copy-start(bf16[320,640]{1,0:T(8,128)(2,1)S(1)} %get-tuple-element.17.refs_0_) | copy-start | bytes 1228804
  83.9 70.1 %copy-start.5 = (bf16[320,640]{1,0:T(8,128)(2,1)}, bf16[320,640]{1,0:T(8,128)(2,1)S(1)}, u32[]{:S(2)}) copy-start(bf16[320,640]{1,0:T(8,128)(2,1)S(1)} %get-tuple-element.16.refs_0_) | copy-start | bytes 1228804
  83.9 12.3 %collective-permute-start.11 = (bf16[320,640]{1,0:T(8,128)(2,1)S(1)}, bf16[320,640]{1,0:T(8,128)(2,1)S(1)}, u32[]{:S(2)}, u32[]{:S(2)}) collective-permute-start(bf16[320,640]{1,0:T(8,128)(2,1)S(1)} %get-tuple-element.17.refs_0_), channel_id=1, source_target_pairs={{0,1},{1,2},{2,3},{3,4},{4,5},{5,6},{6,7},{7,0},{8,9},{9,10},{10,1... | collective-permute-start | bytes 1228808 | tf_op jit(solution)/shard_map/ppermute | solution.py:31
  84.0 12.2 %collective-permute-start.15 = (bf16[320,640]{1,0:T(8,128)(2,1)S(1)}, bf16[320,640]{1,0:T(8,128)(2,1)S(1)}, u32[]{:S(2)}, u32[]{:S(2)}) collective-permute-start(bf16[320,640]{1,0:T(8,128)(2,1)S(1)} %get-tuple-element.16.refs_0_), channel_id=1, source_target_pairs={{0,7},{1,0},{2,1},{3,2},{4,3},{5,4},{6,5},{7,6},{8,15},{9,8},{10,9... | collective-permute-start | bytes 1228808 | tf_op jit(solution)/shard_map/ppermute | solution.py:32
  86.7 17.3 %collective-permute-start.8 = (bf16[320,640]{1,0:T(8,128)(2,1)S(1)}, bf16[320,640]{1,0:T(8,128)(2,1)S(1)}, u32[]{:S(2)}, u32[]{:S(2)}) collective-permute-start(bf16[320,640]{1,0:T(8,128)(2,1)S(1)} %get-tuple-element.17.refs_0_), channel_id=1, source_target_pairs={{0,7},{1,0},{2,1},{3,2},{4,3},{5,4},{6,5},{7,6},{8,15},{9,8},{10,9... | collective-permute-start | bytes 1228808 | tf_op jit(solution)/shard_map/ppermute | solution.py:32
  86.7 27.2 %collective-permute-start.19 = (bf16[320,640]{1,0:T(8,128)(2,1)S(1)}, bf16[320,640]{1,0:T(8,128)(2,1)S(1)}, u32[]{:S(2)}, u32[]{:S(2)}) collective-permute-start(bf16[320,640]{1,0:T(8,128)(2,1)S(1)} %get-tuple-element.16.refs_0_), channel_id=1, source_target_pairs={{0,1},{1,2},{2,3},{3,4},{4,5},{5,6},{6,7},{7,0},{8,9},{9,10},{10,1... | collective-permute-start | bytes 1228808 | tf_op jit(solution)/shard_map/ppermute | solution.py:31
  96.2 17.7 %copy-start.14 = (bf16[320,640]{1,0:T(8,128)(2,1)}, bf16[320,640]{1,0:T(8,128)(2,1)S(1)}, u32[]{:S(2)}) copy-start(bf16[320,640]{1,0:T(8,128)(2,1)S(1)} %collective-permute-done.11.refs_7_) | copy-start | bytes 1228804
  96.2 17.7 %collective-permute-start.12 = (bf16[320,640]{1,0:T(8,128)(2,1)S(1)}, bf16[320,640]{1,0:T(8,128)(2,1)}, u32[]{:S(2)}, u32[]{:S(2)}) collective-permute-start(bf16[320,640]{1,0:T(8,128)(2,1)S(1)} %collective-permute-done.11.refs_7_), channel_id=1, source_target_pairs={{0,1},{1,2},{2,3},{3,4},{4,5},{5,6},{6,7},{7,0},{8,9},{9,10},{10,1... | collective-permute-start | bytes 1228808 | tf_op jit(solution)/shard_map/ppermute | solution.py:31
  96.3 57.8 %copy-start.7 = (bf16[320,640]{1,0:T(8,128)(2,1)}, bf16[320,640]{1,0:T(8,128)(2,1)S(1)}, u32[]{:S(2)}) copy-start(bf16[320,640]{1,0:T(8,128)(2,1)S(1)} %collective-permute-done.15.refs_1_) | copy-start | bytes 1228804
  96.3 17.8 %collective-permute-start.16 = (bf16[320,640]{1,0:T(8,128)(2,1)S(1)}, bf16[320,640]{1,0:T(8,128)(2,1)S(1)}, u32[]{:S(2)}, u32[]{:S(2)}) collective-permute-start(bf16[320,640]{1,0:T(8,128)(2,1)S(1)} %collective-permute-done.15.refs_1_), channel_id=1, source_target_pairs={{0,7},{1,0},{2,1},{3,2},{4,3},{5,4},{6,5},{7,6},{8,15},{9,8},{10,9... | collective-permute-start | bytes 1228808 | tf_op jit(solution)/shard_map/ppermute | solution.py:32
  104.0 23.9 %copy-start.15 = (bf16[320,640]{1,0:T(8,128)(2,1)}, bf16[320,640]{1,0:T(8,128)(2,1)S(1)}, u32[]{:S(2)}) copy-start(bf16[320,640]{1,0:T(8,128)(2,1)S(1)} %collective-permute-done.8.refs_1_) | copy-start | bytes 1228804
  104.0 17.6 %collective-permute-start.9 = (bf16[320,640]{1,0:T(8,128)(2,1)S(1)}, bf16[320,640]{1,0:T(8,128)(2,1)}, u32[]{:S(2)}, u32[]{:S(2)}) collective-permute-start(bf16[320,640]{1,0:T(8,128)(2,1)S(1)} %collective-permute-done.8.refs_1_), channel_id=1, source_target_pairs={{0,7},{1,0},{2,1},{3,2},{4,3},{5,4},{6,5},{7,6},{8,15},{9,8},{10,9... | collective-permute-start | bytes 1228808 | tf_op jit(solution)/shard_map/ppermute | solution.py:32
  113.9 11.7 %collective-permute-start.13 = (bf16[320,640]{1,0:T(8,128)(2,1)}, bf16[320,640]{1,0:T(8,128)(2,1)}, u32[]{:S(2)}, u32[]{:S(2)}) collective-permute-start(bf16[320,640]{1,0:T(8,128)(2,1)} %collective-permute-done.12.refs_6_), channel_id=1, source_target_pairs={{0,1},{1,2},{2,3},{3,4},{4,5},{5,6},{6,7},{7,0},{8,9},{9,10},{10,1... | collective-permute-start | bytes 1228808 | tf_op jit(solution)/shard_map/ppermute | solution.py:31
  113.9 40.1 %copy-start.8 = (bf16[320,640]{1,0:T(8,128)(2,1)}, bf16[320,640]{1,0:T(8,128)(2,1)S(1)}, u32[]{:S(2)}) copy-start(bf16[320,640]{1,0:T(8,128)(2,1)S(1)} %collective-permute-done.19.refs_7_) | copy-start | bytes 1228804
  113.9 20.3 %collective-permute-start.20 = (bf16[320,640]{1,0:T(8,128)(2,1)S(1)}, bf16[320,640]{1,0:T(8,128)(2,1)S(1)}, u32[]{:S(2)}, u32[]{:S(2)}) collective-permute-start(bf16[320,640]{1,0:T(8,128)(2,1)S(1)} %collective-permute-done.19.refs_7_), channel_id=1, source_target_pairs={{0,1},{1,2},{2,3},{3,4},{4,5},{5,6},{6,7},{7,0},{8,9},{9,10},{10,1... | collective-permute-start | bytes 1228808 | tf_op jit(solution)/shard_map/ppermute | solution.py:31
  114.1 40.0 %copy-start.9 = (bf16[320,640]{1,0:T(8,128)(2,1)}, bf16[320,640]{1,0:T(8,128)(2,1)S(1)}, u32[]{:S(2)}) copy-start(bf16[320,640]{1,0:T(8,128)(2,1)S(1)} %collective-permute-done.16.refs_2_) | copy-start | bytes 1228804
  114.1 20.2 %collective-permute-start.17 = (bf16[320,640]{1,0:T(8,128)(2,1)S(1)}, bf16[320,640]{1,0:T(8,128)(2,1)S(1)}, u32[]{:S(2)}, u32[]{:S(2)}) collective-permute-start(bf16[320,640]{1,0:T(8,128)(2,1)S(1)} %collective-permute-done.16.refs_2_), channel_id=1, source_target_pairs={{0,7},{1,0},{2,1},{3,2},{4,3},{5,4},{6,5},{7,6},{8,15},{9,8},{10,9... | collective-permute-start | bytes 1228808 | tf_op jit(solution)/shard_map/ppermute | solution.py:32
  121.6 17.6 %collective-permute-start.10 = (bf16[320,640]{1,0:T(8,128)(2,1)}, bf16[320,640]{1,0:T(8,128)(2,1)}, u32[]{:S(2)}, u32[]{:S(2)}) collective-permute-start(bf16[320,640]{1,0:T(8,128)(2,1)} %collective-permute-done.9.refs_2_), channel_id=1, source_target_pairs={{0,7},{1,0},{2,1},{3,2},{4,3},{5,4},{6,5},{7,6},{8,15},{9,8},{10,9... | collective-permute-start | bytes 1228808 | tf_op jit(solution)/shard_map/ppermute | solution.py:32
  125.6 17.6 %collective-permute-start.14 = (bf16[320,640]{1,0:T(8,128)(2,1)}, bf16[320,640]{1,0:T(8,128)(2,1)}, u32[]{:S(2)}, u32[]{:S(2)}) collective-permute-start(bf16[320,640]{1,0:T(8,128)(2,1)} %collective-permute-done.13.refs_5_), channel_id=1, source_target_pairs={{0,1},{1,2},{2,3},{3,4},{4,5},{5,6},{6,7},{7,0},{8,9},{9,10},{10,1... | collective-permute-start | bytes 1228808 | tf_op jit(solution)/shard_map/ppermute | solution.py:36
  134.3 19.8 %copy-start.10 = (bf16[320,640]{1,0:T(8,128)(2,1)}, bf16[320,640]{1,0:T(8,128)(2,1)S(1)}, u32[]{:S(2)}) copy-start(bf16[320,640]{1,0:T(8,128)(2,1)S(1)} %collective-permute-done.20.refs_6_) | copy-start | bytes 1228804
  134.3 19.8 %collective-permute-start.21 = (bf16[320,640]{1,0:T(8,128)(2,1)S(1)}, bf16[320,640]{1,0:T(8,128)(2,1)S(1)}, u32[]{:S(2)}, u32[]{:S(2)}) collective-permute-start(bf16[320,640]{1,0:T(8,128)(2,1)S(1)} %collective-permute-done.20.refs_6_), channel_id=1, source_target_pairs={{0,1},{1,2},{2,3},{3,4},{4,5},{5,6},{6,7},{7,0},{8,9},{9,10},{10,1... | collective-permute-start | bytes 1228808 | tf_op jit(solution)/shard_map/ppermute | solution.py:31
  134.3 19.8 %copy-start.11 = (bf16[320,640]{1,0:T(8,128)(2,1)}, bf16[320,640]{1,0:T(8,128)(2,1)S(1)}, u32[]{:S(2)}) copy-start(bf16[320,640]{1,0:T(8,128)(2,1)S(1)} %collective-permute-done.17.refs_3_) | copy-start | bytes 1228804
  134.3 19.8 %collective-permute-start.18 = (bf16[320,640]{1,0:T(8,128)(2,1)S(1)}, bf16[320,640]{1,0:T(8,128)(2,1)}, u32[]{:S(2)}, u32[]{:S(2)}) collective-permute-start(bf16[320,640]{1,0:T(8,128)(2,1)S(1)} %collective-permute-done.17.refs_3_), channel_id=1, source_target_pairs={{0,7},{1,0},{2,1},{3,2},{4,3},{5,4},{6,5},{7,6},{8,15},{9,8},{10,9... | collective-permute-start | bytes 1228808 | tf_op jit(solution)/shard_map/ppermute | solution.py:38
  163.0 30.3 %copy-start.1 = (bf16[640,256]{1,0:T(8,128)(2,1)S(1)}, bf16[640,256]{1,0:T(8,128)(2,1)}, u32[]{:S(2)}) copy-start(bf16[640,256]{1,0:T(8,128)(2,1)} %get-tuple-element.13.own) | copy-start | bytes 983044
  163.0 6.6 %collective-permute-start.24 = (bf16[640,256]{1,0:T(8,128)(2,1)}, bf16[640,256]{1,0:T(8,128)(2,1)S(1)}, u32[]{:S(2)}, u32[]{:S(2)}) collective-permute-start(bf16[640,256]{1,0:T(8,128)(2,1)} %get-tuple-element.13.own), channel_id=1, source_target_pairs={{0,112},{8,120},{16,0},{24,8},{32,16},{40,24},{48,32},{56,40},{64,... | collective-permute-start | bytes 983048 | tf_op jit(solution)/shard_map/ppermute | solution.py:32
  163.1 7.9 %collective-permute-start.22 = (bf16[640,256]{1,0:T(8,128)(2,1)}, bf16[640,256]{1,0:T(8,128)(2,1)S(1)}, u32[]{:S(2)}, u32[]{:S(2)}) collective-permute-start(bf16[640,256]{1,0:T(8,128)(2,1)} %get-tuple-element.13.own), channel_id=1, source_target_pairs={{0,16},{8,24},{16,32},{24,40},{32,48},{40,56},{48,64},{56,72},{64,... | collective-permute-start | bytes 983048 | tf_op jit(solution)/shard_map/ppermute | solution.py:31
  169.6 6.7 %collective-permute-start.25 = (bf16[640,256]{1,0:T(8,128)(2,1)S(1)}, bf16[640,256]{1,0:T(8,128)(2,1)S(1)}, u32[]{:S(2)}, u32[]{:S(2)}) collective-permute-start(bf16[640,256]{1,0:T(8,128)(2,1)S(1)} %collective-permute-done.24), channel_id=1, source_target_pairs={{0,112},{8,120},{16,0},{24,8},{32,16},{40,24},{48,32},{56,40},{64,... | collective-permute-start | bytes 983048 | tf_op jit(solution)/shard_map/ppermute | solution.py:32
  171.1 8.1 %collective-permute-start.27 = (bf16[640,256]{1,0:T(8,128)(2,1)S(1)}, bf16[640,256]{1,0:T(8,128)(2,1)S(1)}, u32[]{:S(2)}, u32[]{:S(2)}) collective-permute-start(bf16[640,256]{1,0:T(8,128)(2,1)S(1)} %collective-permute-done.22.far), channel_id=1, source_target_pairs={{0,16},{8,24},{16,32},{24,40},{32,48},{40,56},{48,64},{56,72},{64,... | collective-permute-start | bytes 983048 | tf_op jit(solution)/shard_map/ppermute | solution.py:31
  176.3 7.9 %collective-permute-start.26 = (bf16[640,256]{1,0:T(8,128)(2,1)S(1)}, bf16[640,256]{1,0:T(8,128)(2,1)S(1)}, u32[]{:S(2)}, u32[]{:S(2)}) collective-permute-start(bf16[640,256]{1,0:T(8,128)(2,1)S(1)} %collective-permute-done.25), channel_id=1, source_target_pairs={{0,112},{8,120},{16,0},{24,8},{32,16},{40,24},{48,32},{56,40},{64,... | collective-permute-start | bytes 983048 | tf_op jit(solution)/shard_map/ppermute | solution.py:32
  179.2 7.2 %collective-permute-start.28 = (bf16[640,256]{1,0:T(8,128)(2,1)S(1)}, bf16[640,256]{1,0:T(8,128)(2,1)S(1)}, u32[]{:S(2)}, u32[]{:S(2)}) collective-permute-start(bf16[640,256]{1,0:T(8,128)(2,1)S(1)} %collective-permute-done.27), channel_id=1, source_target_pairs={{0,16},{8,24},{16,32},{24,40},{32,48},{40,56},{48,64},{56,72},{64,... | collective-permute-start | bytes 983048 | tf_op jit(solution)/shard_map/ppermute | solution.py:31
  186.6 38.3 %collective-permute-start.29 = (bf16[4480,256]{1,0:T(8,128)(2,1)S(1)}, bf16[4480,256]{1,0:T(8,128)(2,1)}, u32[]{:S(2)}, u32[]{:S(2)}) collective-permute-start(bf16[4480,256]{1,0:T(8,128)(2,1)S(1)} %constant_dynamic-update-slice_fusion.mine), channel_id=1, source_target_pairs={{0,8},{8,0},{16,24},{24,16},{32,40},{40,32},{48,56},{56,48},{64,72... | collective-permute-start | bytes 6881288 | tf_op jit(solution)/shard_map/ppermute | solution.py:44
  193.3 11.7 %collective-permute-start.23 = (bf16[640,256]{1,0:T(8,128)(2,1)S(1)}, bf16[640,256]{1,0:T(8,128)(2,1)S(1)}, u32[]{:S(2)}, u32[]{:S(2)}) collective-permute-start(bf16[640,256]{1,0:T(8,128)(2,1)S(1)} %copy-done.1), channel_id=1, source_target_pairs={{0,8},{8,16},{16,24},{24,32},{32,40},{40,48},{48,56},{56,64},{64,7... | collective-permute-start | bytes 983048 | tf_op jit(solution)/shard_map/ppermute | solution.py:469
  195.4 9.7 %copy-start.4 = (bf16[5,320,128]{2,1,0:T(8,128)(2,1)S(1)}, bf16[5,320,128]{2,1,0:T(8,128)(2,1)}, u32[]{:S(2)}) copy-start(bf16[5,320,128]{2,1,0:T(8,128)(2,1)} %get-tuple-element.10.q_a) | copy-start | bytes 1228804
  204.9 9.1 %collective-permute-start.30 = (bf16[640,256]{1,0:T(8,128)(2,1)}, bf16[640,256]{1,0:T(8,128)(2,1)S(1)}, u32[]{:S(2)}, u32[]{:S(2)}) collective-permute-start(bf16[640,256]{1,0:T(8,128)(2,1)} %copy-done.16), channel_id=1, source_target_pairs={{0,112},{8,120},{16,0},{24,8},{32,16},{40,24},{48,32},{56,40},{64,... | collective-permute-start | bytes 983048 | tf_op jit(solution)/shard_map/ppermute | solution.py:38
  214.0 10.9 %collective-permute-start.31 = (bf16[640,256]{1,0:T(8,128)(2,1)S(1)}, bf16[640,256]{1,0:T(8,128)(2,1)S(1)}, u32[]{:S(2)}, u32[]{:S(2)}) collective-permute-start(bf16[640,256]{1,0:T(8,128)(2,1)S(1)} %collective-permute-done.30.mine_mid), channel_id=1, source_target_pairs={{0,8},{8,0},{16,24},{24,16},{32,40},{40,32},{48,56},{56,48},{64,72... | collective-permute-start | bytes 983048 | tf_op jit(solution)/shard_map/ppermute | solution.py:44
  222.3 2.6 %copy-start.2 = (s32[4]{0:T(128)S(1)}, s32[4]{0:T(128)}, u32[]{:S(2)}) copy-start(s32[4]{0:T(128)} %pad_add_fusion.1.place) | copy-start | bytes 52
  222.3 2.6 %copy-start.3 = (s32[1,32]{1,0:T(1,128)S(1)}, s32[1,32]{1,0:T(1,128)}, u32[]{:S(2)}) copy-start(s32[1,32]{1,0:T(1,128)} %table.1) | copy-start | bytes 388
  (3 other events, 4.2 us)
where the time goes:
time: 229 us; the launch traced here: 228 us
  waiting for transfers between devices  93.1 us (41%)
  starting transfers between devices  68.4 us (30%)
  Pallas kernels  47.1 us (21%)
  local copies, waits for them, and re-layouts  9.31 us (4%)
  other arithmetic  9.1 us (4%)
    ppermute x12, waiting for transfers between devices, ring(): up = lax.ppermute(up, axis, ahead)  50.5 us
    ppermute x12, starting transfers between devices, ring(): down = lax.ppermute(down, axis, back)  37.8 us
    pallas_call x3, Pallas kernels, project(): pl.pallas_call(kernel, out_shape=tuple(outs), in_specs=specs, out_specs=t...  28.6 us
    ppermute x12, waiting for transfers between devices, ring(): down = lax.ppermute(down, axis, back)  23.9 us
    ppermute x3, starting transfers between devices, swap(): return lax.ppermute(block, axis, [(i, i ^ 1) for i in range(size)])  19.1 us
    ppermute x2, waiting for transfers between devices, ring(): got[count // 2] = lax.ppermute(up, axis, ahead)  16.7 us
    pallas_call x3, Pallas kernels, attend(): pl.pallas_call(functools.partial(attend_kernel, lo=lo, hi=hi), out_shape=...  15.4 us
    unnamed x50, local copies, waits for them, and re-layouts  8.17 us
  transfers between devices with their start and end apart: 32, of which 17 were waited for; matrix products, arithmetic and copies ran while one was open for 5% of the time, Pallas kernels for 16%

commit v1 on v0

--- a/solution.py
+++ b/solution.py
@@ -44,98 +44,81 @@
     return lax.ppermute(block, axis, [(i, i ^ 1) for i in range(size)])
 
 
-def proj_kernel(place, *refs, count, rows, feat, width, lo, n_q, kv, has_scale, has_old):
-    x_refs = refs[:count]
-    mine, other, gain, cos, sin = refs[count : count + 5]
-    at = count + 5
-    old = scale_in = None
+def proj_kernel(place, *refs, count, rows, feat, width, lo, n_q, kv, normed, hand_on, has_old):
+    n_x = 1 if normed else count
+    x_refs = refs[:n_x]
+    mine, other, mine_mid, other_mid, gain, cos, sin = refs[n_x : n_x + 7]
+    at = n_x + 7
+    old = None
     if has_old:
         old = refs[at]
         at += 1
-    if has_scale:
-        scale_in = refs[at]
-        at += 1
-    n_out = (1 if n_q else 0) + (1 if kv else 0) + (0 if has_scale else 1)
+    n_out = (1 if n_q else 0) + (1 if kv else 0) + (1 if hand_on else 0)
     outs = refs[at : at + n_out]
-    xbuf, wbuf, acc, scale_ref, sem_x, sem_w = refs[at + n_out :]
+    xbuf, wbuf, acc, scale_ref, sem_x, sem_w, sem_out = refs[at + n_out :]
     tp, chip, core = place[0], place[1], place[2]
     w_rows = feat // 2
+    mid = count // 2
     tile = 64
 
-    def x_copy(i, src):
-        spot = pl.multiple_of(i * feat, 128)
-        return pltpu.make_async_copy(src, xbuf.at[:, pl.ds(spot, feat)], sem_x.at[i])
-
-    def w_copy(i, which):
-        src = mine if which == 0 else other
+    def x_copy(i):
+        if normed:
+            return pltpu.make_async_copy(x_refs[0], xbuf, sem_x.at[0])
+        return pltpu.make_async_copy(x_refs[i], xbuf.at[:, pl.ds(i * feat, feat)], sem_x.at[i])
+
+    def w_copy(rel, which):
         spot = core if which == 0 else 1 - core
-        rel = jnp.bitwise_and(tp + i - chip, count - 1)
+        if rel == mid:
+            src = mine_mid if which == 0 else other_mid
+        else:
+            src = (mine if which == 0 else other).at[rel if rel < mid else rel - 1]
+        i = jnp.bitwise_and(chip + rel - tp, count - 1)
         return pltpu.make_async_copy(
-            src.at[rel, pl.ds(0, w_rows), pl.ds(lo, width)],
+            src.at[pl.ds(0, w_rows), pl.ds(lo, width)],
             wbuf.at[pl.ds(pl.multiple_of(i * feat + spot * w_rows, 64), w_rows)],
-            sem_w.at[2 * i + which],
+            sem_w.at[2 * rel + which],
         )
 
-    for i in range(count):
-        x_copy(i, x_refs[i]).start()
-
-    def fetch(i, unused):
-        w_copy(i, 0).start()
-        w_copy(i, 1).start()
-        return unused
-
-    lax.fori_loop(0, count, fetch, 0)
-    acc[...] = jnp.zeros_like(acc)
-    if has_scale:
-        scale_ref[...] = scale_in[...]
-    else:
-        scale_ref[...] = jnp.zeros_like(scale_ref)
-
-        def add_piece(i, unused):
-            x_copy(i, x_refs[0]).wait()
-
-            def add_squares(r, unused):
-                at_rows = pl.ds(pl.multiple_of(r * tile, tile), tile)
-                total = scale_ref[at_rows]
-                for g in range(feat // 128):
-                    at_col = pl.ds(pl.multiple_of(i * feat + g * 128, 128), 128)
-                    part = xbuf[at_rows, at_col].astype(jnp.float32)
-                    total = total + part * part
-                scale_ref[at_rows] = total
-                return unused
-
-            return lax.fori_loop(0, rows // tile, add_squares, unused)
-
-        lax.fori_loop(0, count, add_piece, 0)
+    for i in range(n_x):
+        x_copy(i).start()
+    for rel in range(count):
+        w_copy(rel, 0).start()
+        w_copy(rel, 1).start()
+    for i in range(n_x):
+        x_copy(i).wait()
+    hand = None
+    if not normed:
+
+        def add_squares(r, unused):
+            at_rows = pl.ds(pl.multiple_of(r * tile, tile), tile)
+            totals = [jnp.zeros((tile, 128), jnp.float32) for _ in range(2)]
+            for g in range(count * feat // 128):
+                part = xbuf[at_rows, g * 128 : (g + 1) * 128].astype(jnp.float32)
+                totals[g % 2] = totals[g % 2] + part * part
+            scale_ref[at_rows] = totals[0] + totals[1]
+            return unused
+
+        lax.fori_loop(0, rows // tile, add_squares, 0)
         mean = jnp.sum(scale_ref[...], axis=1, keepdims=True) * (1.0 / (feat * count))
         scale_ref[...] = jnp.broadcast_to(lax.rsqrt(mean + EPSILON), scale_ref.shape)
-        outs[-1][...] = scale_ref[...]
-
-    def multiply(c, unused):
-        for k in range(2):
-            i = 2 * c + k
-            feature = jnp.bitwise_and(tp + i, count - 1)
-            if has_scale:
-                x_copy(i, x_refs[0]).wait()
-
-            def normalize(r, unused):
-                at_rows = pl.ds(pl.multiple_of(r * tile, tile), tile)
-                scale = scale_ref[at_rows]
-                for g in range(feat // 128):
-                    at_col = pl.ds(pl.multiple_of(i * feat + g * 128, 128), 128)
-                    part = xbuf[at_rows, at_col].astype(jnp.float32)
-                    by = gain[feature, :, g * 128 : (g + 1) * 128]
-                    xbuf[at_rows, at_col] = (part * scale * by).astype(jnp.bfloat16)
-                return unused
-
-            lax.fori_loop(0, rows // tile, normalize, 0)
-            w_copy(i, 0).wait()
-            w_copy(i, 1).wait()
-        span = pl.ds(pl.multiple_of(c * 2 * feat, 256), 2 * feat)
-        acc[...] += jnp.dot(xbuf[:, span], wbuf[span], preferred_element_type=jnp.float32)
-        return unused
-
-    lax.fori_loop(0, count // 2, multiply, 0)
+
+        def normalize(r, unused):
+            at_rows = pl.ds(pl.multiple_of(r * tile, tile), tile)
+            scale = scale_ref[at_rows]
+            for g in range(count * feat // 128):
+                at_col = slice(g * 128, (g + 1) * 128)
+                part = xbuf[at_rows, at_col].astype(jnp.float32)
+                xbuf[at_rows, at_col] = (part * scale * gain[:, at_col]).astype(jnp.bfloat16)
+            return unused
+
+        lax.fori_loop(0, rows // tile, normalize, 0)
+    for rel in range(count):
+        w_copy(rel, 0).wait()
+        w_copy(rel, 1).wait()
+    acc[...] = jnp.dot(xbuf[...], wbuf[...], preferred_element_type=jnp.float32)
+    if hand_on:
+        hand = pltpu.make_async_copy(xbuf, outs[-1], sem_out)
+        hand.start()
     cosine = cos[...]
     sine = sin[...]
 
@@ -154,20 +137,28 @@
         k_at = n_q * HD
         out[base : base + rows, :HD] = rotated(k_at)
         out[base : base + rows, HD:] = acc[:, k_at + HD : k_at + 2 * HD].astype(jnp.bfloat16)
-
-
-def project(place, pieces, mine, other, gain, cos, sin, n_q, kv, lo, old=None, scale=None):
-    count = len(pieces)
-    rows, feat = pieces[0].shape
+    if hand_on:
+        hand.wait()
+
+
+def project(place, pieces, weights, gain, cos, sin, n_q, kv, lo, old=None, hand_on=False):
+    normed = len(pieces) == 1
+    count = weights[0].shape[0] + 1
+    rows = pieces[0].shape[0]
+    feat = pieces[0].shape[1] // (count if normed else 1)
     width = n_q * HD + (2 * HD if kv else 0)
     outs = []
+    out_specs = []
     if n_q:
         outs.append(jax.ShapeDtypeStruct((n_q, rows, HD), jnp.bfloat16))
+        out_specs.append(pl.BlockSpec(memory_space=VMEM))
     if kv:
         extra = old.shape[0] if old is not None else 0
         outs.append(jax.ShapeDtypeStruct((rows + extra, 2 * HD), jnp.bfloat16))
-    if scale is None:
-        outs.append(jax.ShapeDtypeStruct((rows, 128), jnp.float32))
+        out_specs.append(pl.BlockSpec(memory_space=VMEM))
+    if hand_on:
+        outs.append(jax.ShapeDtypeStruct((rows, count * feat), jnp.bfloat16))
+        out_specs.append(pl.BlockSpec(memory_space=pl.ANY))
     kernel = functools.partial(
         proj_kernel,
         count=count,
@@ -177,29 +168,30 @@
         lo=lo,
         n_q=n_q,
         kv=kv,
-        has_scale=scale is not None,
+        normed=normed,
+        hand_on=hand_on,
         has_old=old is not None,
     )
-    operands = [place, *pieces, mine, other, gain, cos, sin]
+    operands = [place, *pieces, *weights, gain, cos, sin]
     specs = [pl.BlockSpec(memory_space=SMEM)]
-    specs += [pl.BlockSpec(memory_space=pl.ANY)] * (count + 2)
+    specs += [pl.BlockSpec(memory_space=pl.ANY)] * (len(pieces) + 4)
     specs += [pl.BlockSpec(memory_space=VMEM)] * 3
-    for more in (old, scale):
-        if more is not None:
-            operands.append(more)
-            specs.append(pl.BlockSpec(memory_space=VMEM))
+    if old is not None:
+        operands.append(old)
+        specs.append(pl.BlockSpec(memory_space=VMEM))
     return pl.pallas_call(
         kernel,
         out_shape=tuple(outs),
         in_specs=specs,
-        out_specs=tuple(pl.BlockSpec(memory_space=VMEM) for _ in outs),
+        out_specs=tuple(out_specs),
         scratch_shapes=[
             pltpu.VMEM((rows, count * feat), jnp.bfloat16),
             pltpu.VMEM((count * feat, width), jnp.bfloat16),
             pltpu.VMEM((rows, width), jnp.float32),
             pltpu.VMEM((rows, 128), jnp.float32),
-            pltpu.SemaphoreType.DMA((count,)),
+            pltpu.SemaphoreType.DMA((len(pieces),)),
             pltpu.SemaphoreType.DMA((2 * count,)),
+            pltpu.SemaphoreType.DMA,
         ],
         compiler_params=pltpu.CompilerParams(vmem_limit_bytes=VMEM_ALL),
         cost_estimate=pl.CostEstimate(
@@ -270,24 +262,20 @@
             bias = jnp.where(inside, 0.0, -1e30)
             return s[:, :BLOCK] * factor + bias, s[:, BLOCK:] * factor
 
-        for h in range(heads):
-            at = slice(h * BLOCK, (h + 1) * BLOCK)
-            left, right = score(0, h)
-            right = jnp.where(causal, right, -1e30)
-            sbuf[0, at, :BLOCK] = left
-            sbuf[0, at, BLOCK:] = right
-            mbuf[at] = jnp.maximum(left, right)
+        mbuf[...] = jnp.full_like(mbuf, -1e30)
 
         def upward(t, unused):
+            shut = jnp.where(t == 0, -1e30, 0.0)
             for h in range(heads):
                 at = slice(h * BLOCK, (h + 1) * BLOCK)
                 left, right = score(t, h)
+                right = right + jnp.where(causal, 0.0, shut)
                 sbuf[t, at, :BLOCK] = left
                 sbuf[t, at, BLOCK:] = right
                 mbuf[at] = jnp.maximum(mbuf[at], jnp.maximum(left, right))
             return unused
 
-        lax.fori_loop(1, pairs, upward, 0)
+        lax.fori_loop(0, pairs, upward, 0)
         top = jnp.max(mbuf[...], axis=1, keepdims=True)
         mbuf[...] = jnp.broadcast_to(top, mbuf.shape)
         lbuf[...] = jnp.zeros_like(lbuf)
@@ -439,10 +427,19 @@
     w_rows, w_cols = weights.shape
     labels = jnp.pad(owner_map.astype(jnp.bfloat16)[None], ((0, 7), (0, w_cols - local)))
     weights = jnp.concatenate([weights, labels], axis=0)
-    mine = jnp.stack(ring(weights, "dev", 2, True))
-    other = swap(mine, "dev")
-    own_mine = mine[:, w_rows, :local].astype(jnp.int32).reshape(-1)
-    own_other = other[:, w_rows, :local].astype(jnp.int32).reshape(-1)
+    w_got = ring(weights, "dev", 2, True)
+    w_mine = jnp.stack([w_got[i] for i in range(count) if i != mid])
+    w_other = swap(w_mine, "dev")
+    w_other_mid = swap(w_got[mid], "dev")
+    w_set = (w_mine, w_other, w_got[mid], w_other_mid)
+
+    def labels_of(most, middle):
+        by_rel = jnp.concatenate(
+            [most[:mid, w_rows, :local], middle[w_rows : w_rows + 1, :local], most[mid:, w_rows, :local]]
+        )
+        return by_rel.astype(jnp.int32).reshape(-1)
+
+    own_mine, own_other = labels_of(w_mine, w_got[mid]), labels_of(w_other, w_other_mid)
     place, own_mine, own_other = lax.optimization_barrier((place, own_mine, own_other))
 
     token_rows = device * tok + jnp.arange(tok, dtype=jnp.int32)
@@ -455,16 +452,16 @@
     cosine, sine = jnp.cos(angles), jnp.sin(angles)
     cos = jnp.concatenate([cosine, cosine], axis=1)
     sin = jnp.concatenate([-sine, sine], axis=1)
-    gain = norm_gain.astype(jnp.float32).reshape(n_tp, 1, feat)
+    gain = norm_gain.astype(jnp.float32).reshape(n_tp, feat)
+    turn = lax.rem(lax.axis_index("tp") + jnp.arange(n_tp), n_tp)
+    gain = jnp.take(gain, turn, axis=0, mode="clip").reshape(1, n_tp * feat)
 
     q_width = heads * HD
-    q_a, kv_a, _ = project(place, x_a, mine, other, gain, cos[:part], sin[:part], heads, True, 0)
-    kv, scale_b = project(
-        place, x_b, mine, other, gain, cos[part:], sin[part:], 0, True, q_width, old=kv_a
+    q_a, kv_a = project(place, x_a, w_set, gain, cos[:part], sin[:part], heads, True, 0)
+    kv, normed_b = project(
+        place, x_b, w_set, gain, cos[part:], sin[part:], 0, True, q_width, kv_a, True
     )
-    (q_b,) = project(
-        place, x_b, mine, other, gain, cos[part:], sin[part:], heads, False, 0, scale=scale_b
-    )
+    (q_b,) = project(place, [normed_b], w_set, gain, cos[part:], sin[part:], heads, False, 0)
 
     near = lax.ppermute(kv, "dev", [(i, i + 1) for i in range(n_dev - 1)])
     k_got = ring(kv, "dev", 2, False)

time: 229 us -> 223 us (0.974)
  waiting for transfers between devices: 93.1 us -> 85.5 us
  local copies, waits for them, and re-layouts: 9.31 us -> 14.9 us
  starting transfers between devices: 68.4 us -> 63.7 us
    ppermute x12, waiting for transfers between devices: 23.9 us -> 66.9 us  [ring(): down = lax.ppermute(down, axis, back)]
    ppermute x12, waiting for transfers between devices: 50.5 us -> 14.6 us  [ring(): up = lax.ppermute(up, axis, ahead)]
    ppermute x2, waiting for transfers between devices: 16.7 us -> 2.06 us  [ring(): got[count // 2] = lax.ppermute(up, axis, ahead)]
    ppermute x12, starting transfers between devices: 37.8 us -> 32.7 us  [ring(): down = lax.ppermute(down, axis, back)]
    ppermute x3 -> x4, starting transfers between devices: 19.1 us -> 23.8 us  [swap(): return lax.ppermute(block, axis, [(i, i ^ 1) for i in range(size)])]
    ppermute x12, starting transfers between devices: 6.72 us -> 2.39 us  [ring(): up = lax.ppermute(up, axis, ahead)]
    unnamed x50 -> x58, local copies, waits for them, and re-layouts: 8.17 us -> 9.04 us
  transfers between devices with their start and end apart: 32 -> 33, of which waited for: 17 -> 20; matrix products, arithmetic and copies ran while one was open for 5% -> 8% of each run, Pallas kernels for 16% -> 16%
where the time goes in v1:
time: 223 us; the launch traced here: 222 us
  waiting for transfers between devices  85.5 us (38%)
  starting transfers between devices  63.7 us (29%)
  Pallas kernels  47.3 us (21%)
  local copies, waits for them, and re-layouts  14.9 us (7%)
  other arithmetic  9.44 us (4%)
    ppermute x12, waiting for transfers between devices, ring(): down = lax.ppermute(down, axis, back)  66.9 us
    ppermute x12, starting transfers between devices, ring(): down = lax.ppermute(down, axis, back)  32.7 us
    pallas_call x3, Pallas kernels, project(): pl.pallas_call(kernel, out_shape=tuple(outs), in_specs=specs, out_specs=t...  28.5 us
    ppermute x4, starting transfers between devices, swap(): return lax.ppermute(block, axis, [(i, i ^ 1) for i in range(size)])  23.8 us
    pallas_call x3, Pallas kernels, attend(): pl.pallas_call(functools.partial(attend_kernel, lo=lo, hi=hi), out_shape=...  15.6 us
    ppermute x12, waiting for transfers between devices, ring(): up = lax.ppermute(up, axis, ahead)  14.6 us
    unnamed x58, local copies, waits for them, and re-layouts  9.04 us
  transfers between devices with their start and end apart: 33, of which 20 were waited for; matrix products, arithmetic and copies ran while one was open for 8% of the time, Pallas kernels for 16%

profile of v1, /device:TPU:513, one launch (start us, length us, event | category | flops | bytes accessed | tf_op | source)
XLA Modules:
  0.0 222.1 jit_solution(165924842296793878)
XLA Ops:
  1.3 2.0 constant_dynamic-update-slice_fusion.6
  3.3 12.4 %collective-permute-start = (bf16[328,896]{1,0:T(8,128)(2,1)S(1)}, bf16[328,896]{1,0:T(8,128)(2,1)S(1)}, u32[]{:S(2)}, u32[]{:S(2)}) collective-permute-start(bf16[328,896]{1,0:T(8,128)(2,1)S(1)} %get-tuple-element.17), channel_id=1, source_target_pairs={{0,112},{8,120},{16,0},{24,8},{32,16},{40,24},{48,32},{56,40},{64,... | collective-permute-start | bytes 1763336 | tf_op jit(solution)/shard_map/ppermute | solution.py:32
  15.7 6.8 %collective-permute-done = bf16[328,896]{1,0:T(8,128)(2,1)S(1)} collective-permute-done((bf16[328,896]{1,0:T(8,128)(2,1)S(1)}, bf16[328,896]{1,0:T(8,128)(2,1)S(1)}, u32[]{:S(2)}, u32[]{:S(2)}) %collective-permute-start) | collective-permute-done | bytes 587808 | tf_op jit(solution)/shard_map/ppermute | solution.py:32
  22.5 5.4 %collective-permute-start.1 = (bf16[328,896]{1,0:T(8,128)(2,1)S(1)}, bf16[328,896]{1,0:T(8,128)(2,1)S(1)}, u32[]{:S(2)}, u32[]{:S(2)}) collective-permute-start(bf16[328,896]{1,0:T(8,128)(2,1)S(1)} %collective-permute-done), channel_id=1, source_target_pairs={{0,112},{8,120},{16,0},{24,8},{32,16},{40,24},{48,32},{56,40},{64,... | collective-permute-start | bytes 1763336 | tf_op jit(solution)/shard_map/ppermute | solution.py:32
  27.9 9.1 %collective-permute-done.1 = bf16[328,896]{1,0:T(8,128)(2,1)S(1)} collective-permute-done((bf16[328,896]{1,0:T(8,128)(2,1)S(1)}, bf16[328,896]{1,0:T(8,128)(2,1)S(1)}, u32[]{:S(2)}, u32[]{:S(2)}) %collective-permute-start.1) | collective-permute-done | bytes 587808 | tf_op jit(solution)/shard_map/ppermute | solution.py:32
  37.0 3.1 %collective-permute-start.2 = (bf16[328,896]{1,0:T(8,128)(2,1)S(1)}, bf16[328,896]{1,0:T(8,128)(2,1)S(1)}, u32[]{:S(2)}, u32[]{:S(2)}) collective-permute-start(bf16[328,896]{1,0:T(8,128)(2,1)S(1)} %collective-permute-done.1), channel_id=1, source_target_pairs={{0,112},{8,120},{16,0},{24,8},{32,16},{40,24},{48,32},{56,40},{64,... | collective-permute-start | bytes 1763336 | tf_op jit(solution)/shard_map/ppermute | solution.py:32
  42.9 8.5 %collective-permute-done.2 = bf16[328,896]{1,0:T(8,128)(2,1)S(1)} collective-permute-done((bf16[328,896]{1,0:T(8,128)(2,1)S(1)}, bf16[328,896]{1,0:T(8,128)(2,1)S(1)}, u32[]{:S(2)}, u32[]{:S(2)}) %collective-permute-start.2) | collective-permute-done | bytes 587808 | tf_op jit(solution)/shard_map/ppermute | solution.py:32
  52.4 2.6 %collective-permute-done.5 = bf16[328,896]{1,0:T(8,128)(2,1)S(1)} collective-permute-done((bf16[328,896]{1,0:T(8,128)(2,1)S(1)}, bf16[328,896]{1,0:T(8,128)(2,1)S(1)}, u32[]{:S(2)}, u32[]{:S(2)}) %collective-permute-start.5) | collective-permute-done | bytes 587808 | tf_op jit(solution)/shard_map/ppermute | solution.py:31
  57.7 10.2 %collective-permute-start.7 = (bf16[7,328,896]{2,1,0:T(8,128)(2,1)}, bf16[7,328,896]{2,1,0:T(8,128)(2,1)}, u32[]{:S(2)}, u32[]{:S(2)}) collective-permute-start(bf16[7,328,896]{2,1,0:T(8,128)(2,1)} %constant_dynamic-update-slice_fusion.refs_8_.refs_1_), channel_id=1, source_target_pairs={{0,8},{8,0},{16,24},{24,16},{32,40},{40,32},{48,56},{56,48},{64,72... | collective-permute-start | bytes 12343304 | tf_op jit(solution)/shard_map/ppermute | solution.py:44
  68.7 1.0 collective-permute-start.9
  70.2 2.2 %collective-permute-start.16 = (bf16[320,640]{1,0:T(8,128)(2,1)S(1)}, bf16[320,640]{1,0:T(8,128)(2,1)}, u32[]{:S(2)}, u32[]{:S(2)}) collective-permute-start(bf16[320,640]{1,0:T(8,128)(2,1)S(1)} %get-tuple-element.18.refs_0_), channel_id=1, source_target_pairs={{0,7},{1,0},{2,1},{3,2},{4,3},{5,4},{6,5},{7,6},{8,15},{9,8},{10,9... | collective-permute-start | bytes 1228808 | tf_op jit(solution)/shard_map/ppermute | solution.py:32
  72.6 7.4 %collective-permute-done.9.refs_1_ = bf16[320,640]{1,0:T(8,128)(2,1)} collective-permute-done((bf16[320,640]{1,0:T(8,128)(2,1)}, bf16[320,640]{1,0:T(8,128)(2,1)}, u32[]{:S(2)}, u32[]{:S(2)}) %collective-permute-start.9) | collective-permute-done | bytes 409632 | tf_op jit(solution)/shard_map/ppermute | solution.py:32
  80.1 1.9 collective-permute-done.12.refs_7_
  82.5 6.3 %collective-permute-done.16.refs_1_ = bf16[320,640]{1,0:T(8,128)(2,1)} collective-permute-done((bf16[320,640]{1,0:T(8,128)(2,1)S(1)}, bf16[320,640]{1,0:T(8,128)(2,1)}, u32[]{:S(2)}, u32[]{:S(2)}) %collective-permute-start.16) | collective-permute-done | bytes 409632 | tf_op jit(solution)/shard_map/ppermute | solution.py:32
  88.8 1.9 collective-permute-done.20.refs_7_
  90.8 1.0 collective-permute-start.17
  91.8 2.1 multiply_sine_fusion
  93.9 3.7 %collective-permute-done.10.refs_2_ = bf16[320,640]{1,0:T(8,128)(2,1)} collective-permute-done((bf16[320,640]{1,0:T(8,128)(2,1)}, bf16[320,640]{1,0:T(8,128)(2,1)}, u32[]{:S(2)}, u32[]{:S(2)}) %collective-permute-start.10) | collective-permute-done | bytes 409632 | tf_op jit(solution)/shard_map/ppermute | solution.py:32
  97.6 2.4 %collective-permute-done.13.refs_6_ = bf16[320,640]{1,0:T(8,128)(2,1)} collective-permute-done((bf16[320,640]{1,0:T(8,128)(2,1)}, bf16[320,640]{1,0:T(8,128)(2,1)}, u32[]{:S(2)}, u32[]{:S(2)}) %collective-permute-start.13) | collective-permute-done | bytes 409632 | tf_op jit(solution)/shard_map/ppermute | solution.py:31
  100.0 2.3 %collective-permute-start.8 = (bf16[328,896]{1,0:T(8,128)(2,1)S(1)}, bf16[328,896]{1,0:T(8,128)(2,1)S(1)}, u32[]{:S(2)}, u32[]{:S(2)}) collective-permute-start(bf16[328,896]{1,0:T(8,128)(2,1)S(1)} %collective-permute-done.6.refs_10_.refs_3_), channel_id=1, source_target_pairs={{0,8},{8,0},{16,24},{24,16},{32,40},{40,32},{48,56},{56,48},{64,72... | collective-permute-start | bytes 1763336 | tf_op jit(solution)/shard_map/ppermute | solution.py:44
  103.6 2.7 %collective-permute-done.17.refs_2_ = bf16[320,640]{1,0:T(8,128)(2,1)} collective-permute-done((bf16[320,640]{1,0:T(8,128)(2,1)}, bf16[320,640]{1,0:T(8,128)(2,1)}, u32[]{:S(2)}, u32[]{:S(2)}) %collective-permute-start.17) | collective-permute-done | bytes 409632 | tf_op jit(solution)/shard_map/ppermute | solution.py:32
  106.4 2.2 %collective-permute-start.18 = (bf16[320,640]{1,0:T(8,128)(2,1)}, bf16[320,640]{1,0:T(8,128)(2,1)}, u32[]{:S(2)}, u32[]{:S(2)}) collective-permute-start(bf16[320,640]{1,0:T(8,128)(2,1)} %collective-permute-done.17.refs_2_), channel_id=1, source_target_pairs={{0,7},{1,0},{2,1},{3,2},{4,3},{5,4},{6,5},{7,6},{8,15},{9,8},{10,9... | collective-permute-start | bytes 1228808 | tf_op jit(solution)/shard_map/ppermute | solution.py:32
  109.8 1.9 gather_fusion
  111.7 1.5 copy.16
  113.2 2.4 %pad_maximum_fusion = (f32[320,128]{1,0:T(8,128)}, f32[320,128]{1,0:T(8,128)}, f32[320,128]{1,0:T(8,128)}, f32[320,128]{1,0:T(8,128)}) fusion(f32[640,64]{1,0:T(8,128)} %get-tuple-element.24, f32[640,64]{1,0:T(8,128)} %get-tuple-element.25, f32[640,64]{1,0:T(8,128)} %get-tuple-element.26), kind=kLoop, calls=%fused_computation.12 | loop fusion | flops 163840 | bytes 1146880 | tf_op jit(solution)/shard_map/concatenate | solution.py:454
  115.7 1.9 collective-permute-done.14.refs_5_
  117.8 2.8 %collective-permute-start.19 = (bf16[320,640]{1,0:T(8,128)(2,1)}, bf16[320,640]{1,0:T(8,128)(2,1)S(1)}, u32[]{:S(2)}, u32[]{:S(2)}) collective-permute-start(bf16[320,640]{1,0:T(8,128)(2,1)} %collective-permute-done.18.refs_3_), channel_id=1, source_target_pairs={{0,7},{1,0},{2,1},{3,2},{4,3},{5,4},{6,5},{7,6},{8,15},{9,8},{10,9... | collective-permute-start | bytes 1228808 | tf_op jit(solution)/shard_map/ppermute | solution.py:38
  122.2 3.6 %collective-permute-done.11.refs_3_ = bf16[320,640]{1,0:T(8,128)(2,1)} collective-permute-done((bf16[320,640]{1,0:T(8,128)(2,1)}, bf16[320,640]{1,0:T(8,128)(2,1)}, u32[]{:S(2)}, u32[]{:S(2)}) %collective-permute-start.11) | collective-permute-done | bytes 409632 | tf_op jit(solution)/shard_map/ppermute | solution.py:32
  125.9 2.1 collective-permute-done.15.refs_4_
  127.9 11.6 %shard_map.95 = (bf16[5,320,128]{2,1,0:T(8,128)(2,1)}, bf16[320,256]{1,0:T(8,128)(2,1)}) custom-call(s32[4]{0:T(128)} %pad_add_fusion.1.place, bf16[320,640]{1,0:T(8,128)(2,1)} %get-tuple-element.19.refs_0_, bf16[320,640]{1,0:T(8,128)(2,1)} %collective-permute-done.9.refs_1_, bf16[320,640]{1,0:T(8,128)(2,1)} %collective-permute-done.10.refs_2_, ...), custom_call_target="tpu_custom_call" | custom-call | flops 2936012800 | bytes 12451840 | tf_op jit(solution)/shard_map/pallas_call | solution.py:182
  140.5 8.2 %shard_map.96 = (bf16[640,256]{1,0:T(8,128)(2,1)}, bf16[320,5120]{1,0:T(8,128)(2,1)}) custom-call(s32[4]{0:T(128)} %pad_add_fusion.1.place, bf16[320,640]{1,0:T(8,128)(2,1)} %copy-done.13, bf16[320,640]{1,0:T(8,128)(2,1)} %collective-permute-done.16.refs_1_, bf16[320,640]{1,0:T(8,128)(2,1)} %collective-permute-done.17.refs_2_, ...), custom_call_target="tpu_custom_call" | custom-call | flops 838860800 | bytes 5898240 | tf_op jit(solution)/shard_map/pallas_call | solution.py:182
  150.5 4.7 %collective-permute-done.25 = bf16[640,256]{1,0:T(8,128)(2,1)S(1)} collective-permute-done((bf16[640,256]{1,0:T(8,128)(2,1)}, bf16[640,256]{1,0:T(8,128)(2,1)S(1)}, u32[]{:S(2)}, u32[]{:S(2)}) %collective-permute-start.25) | collective-permute-done | bytes 327712 | tf_op jit(solution)/shard_map/ppermute | solution.py:32
  155.2 1.8 collective-permute-start.26
  157.1 7.7 %collective-permute-done.26 = bf16[640,256]{1,0:T(8,128)(2,1)S(1)} collective-permute-done((bf16[640,256]{1,0:T(8,128)(2,1)S(1)}, bf16[640,256]{1,0:T(8,128)(2,1)S(1)}, u32[]{:S(2)}, u32[]{:S(2)}) %collective-permute-start.26) | collective-permute-done | bytes 327712 | tf_op jit(solution)/shard_map/ppermute | solution.py:32
  164.7 1.9 collective-permute-start.27
  166.6 1.0 constant_dynamic-update-slice_fusion.13
  167.8 6.3 %collective-permute-done.27 = bf16[640,256]{1,0:T(8,128)(2,1)S(1)} collective-permute-done((bf16[640,256]{1,0:T(8,128)(2,1)S(1)}, bf16[640,256]{1,0:T(8,128)(2,1)S(1)}, u32[]{:S(2)}, u32[]{:S(2)}) %collective-permute-start.27) | collective-permute-done | bytes 327712 | tf_op jit(solution)/shard_map/ppermute | solution.py:32
  174.1 3.7 %collective-permute-done.29 = bf16[640,256]{1,0:T(8,128)(2,1)S(1)} collective-permute-done((bf16[640,256]{1,0:T(8,128)(2,1)S(1)}, bf16[640,256]{1,0:T(8,128)(2,1)S(1)}, u32[]{:S(2)}, u32[]{:S(2)}) %collective-permute-start.29) | collective-permute-done | bytes 327712 | tf_op jit(solution)/shard_map/ppermute | solution.py:31
  177.9 9.9 %collective-permute-start.30 = (bf16[4480,256]{1,0:T(8,128)(2,1)S(1)}, bf16[4480,256]{1,0:T(8,128)(2,1)}, u32[]{:S(2)}, u32[]{:S(2)}) collective-permute-start(bf16[4480,256]{1,0:T(8,128)(2,1)S(1)} %constant_dynamic-update-slice_fusion.7.mine), channel_id=1, source_target_pairs={{0,8},{8,0},{16,24},{24,16},{32,40},{40,32},{48,56},{56,48},{64,72... | collective-permute-start | bytes 6881288 | tf_op jit(solution)/shard_map/ppermute | solution.py:44
  187.8 1.9 collective-permute-start.24
  189.9 8.7 %shard_map.97.q_b = bf16[5,320,128]{2,1,0:T(8,128)(2,1)} custom-call(s32[4]{0:T(128)} %pad_add_fusion.1.place, bf16[320,5120]{1,0:T(8,128)(2,1)} %get-tuple-element.12.refs_0_, bf16[7,328,896]{2,1,0:T(8,128)(2,1)} %constant_dynamic-update-slice_fusion.refs_8_.refs_1_, bf16[7,328,896]{2,1,0:T(8,128)(2,1)} %collective-permute-done.7.refs_9_.refs_2_, ...), custom_call_target="tpu_custom_call" | custom-call | flops 2097152000 | bytes 9830400 | tf_op jit(solution)/shard_map/pallas_call | solution.py:182
  198.8 1.0 copy-done
  199.7 6.0 %shard_map.98.refs_0_ = bf16[640,640]{1,0:T(8,128)(2,1)} custom-call(s32[9]{0:T(128)S(1)} %pad_add_fusion.info, bf16[5,320,128]{2,1,0:T(8,128)(2,1)S(1)} %copy-done.4, bf16[5,320,128]{2,1,0:T(8,128)(2,1)S(1)} %copy-done, bf16[640,256]{1,0:T(8,128)(2,1)S(1)} %collective-permute-done.23.far, bf16[640,256]{1,0:T(8,128)(2,1)S(1)} %collective-permute-done.24.near, ...), custom_call_target="tpu_custom_call" | custom-call | flops 4000000000 | bytes 4000000 | tf_op jit(solution)/shard_map/pallas_call | solution.py:314
  205.8 1.9 collective-permute-done.31.mine_mid
  207.7 1.4 collective-permute-start.32
  209.0 7.0 %shard_map.99.refs_0_ = bf16[640,640]{1,0:T(8,128)(2,1)} custom-call(s32[9]{0:T(128)S(1)} %pad_add_fusion.info, bf16[5,320,128]{2,1,0:T(8,128)(2,1)S(1)} %copy-done.4, bf16[5,320,128]{2,1,0:T(8,128)(2,1)S(1)} %copy-done, bf16[640,256]{1,0:T(8,128)(2,1)S(1)} %collective-permute-done.23.far, ...), custom_call_target="tpu_custom_call", output_to_operand_aliasing={{}: (6, {})} | custom-call | flops 4000000000 | bytes 4000000 | tf_op jit(solution)/shard_map/pallas_call | solution.py:314
  216.1 2.6 %shard_map.100 = bf16[640,640]{1,0:T(8,128)(2,1)} custom-call(s32[9]{0:T(128)S(1)} %pad_add_fusion.info, bf16[5,320,128]{2,1,0:T(8,128)(2,1)S(1)} %copy-done.4, bf16[5,320,128]{2,1,0:T(8,128)(2,1)S(1)} %copy-done, bf16[640,256]{1,0:T(8,128)(2,1)S(1)} %collective-permute-done.23.far, ...), custom_call_target="tpu_custom_call", output_to_operand_aliasing={{}: (6, {})} | custom-call | flops 2000000000 | bytes 4000000 | tf_op jit(solution)/shard_map/pallas_call | solution.py:314
  218.7 3.2 %shard_map.101 = bf16[32,128,256]{2,1,0:T(8,128)(2,1)} custom-call(s32[4]{0:T(128)S(1)} %copy-done.2, s32[40]{0:T(128)S(1)} %reshape.93.own_mine, s32[40]{0:T(128)S(1)} %reshape.94.own_other, s32[1,32]{1,0:T(1,128)S(1)} %copy-done.3, bf16[4480,256]{1,0:T(8,128)(2,1)S(1)} %constant_dynamic-update-slice_fusion.7.mine, ...), custom_call_target="tpu_custom_call" | custom-call | tf_op jit(solution)/shard_map/pallas_call | solution.py:398
  (112 shorter events, 16.8 us)
Async XLA Ops:
  3.3 19.2 %collective-permute-start = (bf16[328,896]{1,0:T(8,128)(2,1)S(1)}, bf16[328,896]{1,0:T(8,128)(2,1)S(1)}, u32[]{:S(2)}, u32[]{:S(2)}) collective-permute-start(bf16[328,896]{1,0:T(8,128)(2,1)S(1)} %get-tuple-element.17), channel_id=1, source_target_pairs={{0,112},{8,120},{16,0},{24,8},{32,16},{40,24},{48,32},{56,40},{64,... | collective-permute-start | bytes 1763336 | tf_op jit(solution)/shard_map/ppermute | solution.py:32
  15.7 12.2 %collective-permute-start.3 = (bf16[328,896]{1,0:T(8,128)(2,1)S(1)}, bf16[328,896]{1,0:T(8,128)(2,1)S(1)}, u32[]{:S(2)}, u32[]{:S(2)}) collective-permute-start(bf16[328,896]{1,0:T(8,128)(2,1)S(1)} %get-tuple-element.17), channel_id=1, source_target_pairs={{0,16},{8,24},{16,32},{24,40},{32,48},{40,56},{48,64},{56,72},{64,... | collective-permute-start | bytes 1763336 | tf_op jit(solution)/shard_map/ppermute | solution.py:31
  22.5 33.4 %copy-start.7 = (bf16[328,896]{1,0:T(8,128)(2,1)}, bf16[328,896]{1,0:T(8,128)(2,1)S(1)}, u32[]{:S(2)}) copy-start(bf16[328,896]{1,0:T(8,128)(2,1)S(1)} %collective-permute-done) | copy-start | bytes 1763332
  22.5 14.5 %collective-permute-start.1 = (bf16[328,896]{1,0:T(8,128)(2,1)S(1)}, bf16[328,896]{1,0:T(8,128)(2,1)S(1)}, u32[]{:S(2)}, u32[]{:S(2)}) collective-permute-start(bf16[328,896]{1,0:T(8,128)(2,1)S(1)} %collective-permute-done), channel_id=1, source_target_pairs={{0,112},{8,120},{16,0},{24,8},{32,16},{40,24},{48,32},{56,40},{64,... | collective-permute-start | bytes 1763336 | tf_op jit(solution)/shard_map/ppermute | solution.py:32
  27.9 12.5 %collective-permute-start.4 = (bf16[328,896]{1,0:T(8,128)(2,1)S(1)}, bf16[328,896]{1,0:T(8,128)(2,1)S(1)}, u32[]{:S(2)}, u32[]{:S(2)}) collective-permute-start(bf16[328,896]{1,0:T(8,128)(2,1)S(1)} %collective-permute-done.3), channel_id=1, source_target_pairs={{0,16},{8,24},{16,32},{24,40},{32,48},{40,56},{48,64},{56,72},{64,... | collective-permute-start | bytes 1763336 | tf_op jit(solution)/shard_map/ppermute | solution.py:31
  37.0 18.9 %copy-start.9 = (bf16[328,896]{1,0:T(8,128)(2,1)}, bf16[328,896]{1,0:T(8,128)(2,1)S(1)}, u32[]{:S(2)}) copy-start(bf16[328,896]{1,0:T(8,128)(2,1)S(1)} %collective-permute-done.1) | copy-start | bytes 1763332
  37.0 14.5 %collective-permute-start.2 = (bf16[328,896]{1,0:T(8,128)(2,1)S(1)}, bf16[328,896]{1,0:T(8,128)(2,1)S(1)}, u32[]{:S(2)}, u32[]{:S(2)}) collective-permute-start(bf16[328,896]{1,0:T(8,128)(2,1)S(1)} %collective-permute-done.1), channel_id=1, source_target_pairs={{0,112},{8,120},{16,0},{24,8},{32,16},{40,24},{48,32},{56,40},{64,... | collective-permute-start | bytes 1763336 | tf_op jit(solution)/shard_map/ppermute | solution.py:32
  40.4 14.6 %collective-permute-start.5 = (bf16[328,896]{1,0:T(8,128)(2,1)S(1)}, bf16[328,896]{1,0:T(8,128)(2,1)S(1)}, u32[]{:S(2)}, u32[]{:S(2)}) collective-permute-start(bf16[328,896]{1,0:T(8,128)(2,1)S(1)} %collective-permute-done.4), channel_id=1, source_target_pairs={{0,16},{8,24},{16,32},{24,40},{32,48},{40,56},{48,64},{56,72},{64,... | collective-permute-start | bytes 1763336 | tf_op jit(solution)/shard_map/ppermute | solution.py:31
  42.9 24.9 %copy-start.14 = (bf16[640,640]{1,0:T(8,128)(2,1)S(1)}, bf16[640,640]{1,0:T(8,128)(2,1)}, u32[]{:S(2)}) copy-start(bf16[640,640]{1,0:T(8,128)(2,1)} %param.8) | copy-start | bytes 2457604
  51.5 6.2 %copy-start.11 = (bf16[328,896]{1,0:T(8,128)(2,1)}, bf16[328,896]{1,0:T(8,128)(2,1)S(1)}, u32[]{:S(2)}) copy-start(bf16[328,896]{1,0:T(8,128)(2,1)S(1)} %collective-permute-done.2) | copy-start | bytes 1763332
  55.8 16.5 %copy-start.19 = (s32[8]{0:T(128)S(1)}, s32[8]{0:T(128)}, u32[]{:S(2)}) copy-start(s32[8]{0:T(128)} %param.13) | copy-start | bytes 100
  55.9 53.3 %copy-start.18 = (bf16[5120]{0:T(1024)(128)(2,1)S(1)}, bf16[5120]{0:T(1024)(128)(2,1)}, u32[]{:S(2)}) copy-start(bf16[5120]{0:T(1024)(128)(2,1)} %param.9) | copy-start | bytes 30724
  57.7 63.1 %collective-permute-start.7 = (bf16[7,328,896]{2,1,0:T(8,128)(2,1)}, bf16[7,328,896]{2,1,0:T(8,128)(2,1)}, u32[]{:S(2)}, u32[]{:S(2)}) collective-permute-start(bf16[7,328,896]{2,1,0:T(8,128)(2,1)} %constant_dynamic-update-slice_fusion.refs_8_.refs_1_), channel_id=1, source_target_pairs={{0,8},{8,0},{16,24},{24,16},{32,40},{40,32},{48,56},{56,48},{64,72... | collective-permute-start | bytes 12343304 | tf_op jit(solution)/shard_map/ppermute | solution.py:44
  68.7 31.3 %copy-start.13 = (bf16[320,640]{1,0:T(8,128)(2,1)}, bf16[320,640]{1,0:T(8,128)(2,1)S(1)}, u32[]{:S(2)}) copy-start(bf16[320,640]{1,0:T(8,128)(2,1)S(1)} %get-tuple-element.18.refs_0_) | copy-start | bytes 1228804
  68.7 11.3 %collective-permute-start.9 = (bf16[320,640]{1,0:T(8,128)(2,1)}, bf16[320,640]{1,0:T(8,128)(2,1)}, u32[]{:S(2)}, u32[]{:S(2)}) collective-permute-start(bf16[320,640]{1,0:T(8,128)(2,1)} %get-tuple-element.19.refs_0_), channel_id=1, source_target_pairs={{0,7},{1,0},{2,1},{3,2},{4,3},{5,4},{6,5},{7,6},{8,15},{9,8},{10,9... | collective-permute-start | bytes 1228808 | tf_op jit(solution)/shard_map/ppermute | solution.py:32
  69.7 12.3 %collective-permute-start.12 = (bf16[320,640]{1,0:T(8,128)(2,1)}, bf16[320,640]{1,0:T(8,128)(2,1)}, u32[]{:S(2)}, u32[]{:S(2)}) collective-permute-start(bf16[320,640]{1,0:T(8,128)(2,1)} %get-tuple-element.19.refs_0_), channel_id=1, source_target_pairs={{0,1},{1,2},{2,3},{3,4},{4,5},{5,6},{6,7},{7,0},{8,9},{9,10},{10,1... | collective-permute-start | bytes 1228808 | tf_op jit(solution)/shard_map/ppermute | solution.py:31
  70.2 18.6 %collective-permute-start.16 = (bf16[320,640]{1,0:T(8,128)(2,1)S(1)}, bf16[320,640]{1,0:T(8,128)(2,1)}, u32[]{:S(2)}, u32[]{:S(2)}) collective-permute-start(bf16[320,640]{1,0:T(8,128)(2,1)S(1)} %get-tuple-element.18.refs_0_), channel_id=1, source_target_pairs={{0,7},{1,0},{2,1},{3,2},{4,3},{5,4},{6,5},{7,6},{8,15},{9,8},{10,9... | collective-permute-start | bytes 1228808 | tf_op jit(solution)/shard_map/ppermute | solution.py:32
  72.4 18.4 %collective-permute-start.20 = (bf16[320,640]{1,0:T(8,128)(2,1)S(1)}, bf16[320,640]{1,0:T(8,128)(2,1)}, u32[]{:S(2)}, u32[]{:S(2)}) collective-permute-start(bf16[320,640]{1,0:T(8,128)(2,1)S(1)} %get-tuple-element.18.refs_0_), channel_id=1, source_target_pairs={{0,1},{1,2},{2,3},{3,4},{4,5},{5,6},{6,7},{7,0},{8,9},{9,10},{10,1... | collective-permute-start | bytes 1228808 | tf_op jit(solution)/shard_map/ppermute | solution.py:31
  80.0 20.0 %collective-permute-start.6 = (bf16[328,896]{1,0:T(8,128)(2,1)S(1)}, bf16[328,896]{1,0:T(8,128)(2,1)S(1)}, u32[]{:S(2)}, u32[]{:S(2)}) collective-permute-start(bf16[328,896]{1,0:T(8,128)(2,1)S(1)} %collective-permute-done.5), channel_id=1, source_target_pairs={{0,16},{8,24},{16,32},{24,40},{32,48},{40,56},{48,64},{56,72},{64,... | collective-permute-start | bytes 1763336 | tf_op jit(solution)/shard_map/ppermute | solution.py:36
  82.0 15.6 %collective-permute-start.10 = (bf16[320,640]{1,0:T(8,128)(2,1)}, bf16[320,640]{1,0:T(8,128)(2,1)}, u32[]{:S(2)}, u32[]{:S(2)}) collective-permute-start(bf16[320,640]{1,0:T(8,128)(2,1)} %collective-permute-done.9.refs_1_), channel_id=1, source_target_pairs={{0,7},{1,0},{2,1},{3,2},{4,3},{5,4},{6,5},{7,6},{8,15},{9,8},{10,9... | collective-permute-start | bytes 1228808 | tf_op jit(solution)/shard_map/ppermute | solution.py:32
  88.8 11.2 %collective-permute-start.13 = (bf16[320,640]{1,0:T(8,128)(2,1)}, bf16[320,640]{1,0:T(8,128)(2,1)}, u32[]{:S(2)}, u32[]{:S(2)}) collective-permute-start(bf16[320,640]{1,0:T(8,128)(2,1)} %collective-permute-done.12.refs_7_), channel_id=1, source_target_pairs={{0,1},{1,2},{2,3},{3,4},{4,5},{5,6},{6,7},{7,0},{8,9},{9,10},{10,1... | collective-permute-start | bytes 1228808 | tf_op jit(solution)/shard_map/ppermute | solution.py:31
  90.8 15.6 %collective-permute-start.17 = (bf16[320,640]{1,0:T(8,128)(2,1)}, bf16[320,640]{1,0:T(8,128)(2,1)}, u32[]{:S(2)}, u32[]{:S(2)}) collective-permute-start(bf16[320,640]{1,0:T(8,128)(2,1)} %collective-permute-done.16.refs_1_), channel_id=1, source_target_pairs={{0,7},{1,0},{2,1},{3,2},{4,3},{5,4},{6,5},{7,6},{8,15},{9,8},{10,9... | collective-permute-start | bytes 1228808 | tf_op jit(solution)/shard_map/ppermute | solution.py:32
  97.6 18.0 %collective-permute-start.21 = (bf16[320,640]{1,0:T(8,128)(2,1)}, bf16[320,640]{1,0:T(8,128)(2,1)}, u32[]{:S(2)}, u32[]{:S(2)}) collective-permute-start(bf16[320,640]{1,0:T(8,128)(2,1)} %collective-permute-done.20.refs_7_), channel_id=1, source_target_pairs={{0,1},{1,2},{2,3},{3,4},{4,5},{5,6},{6,7},{7,0},{8,9},{9,10},{10,1... | collective-permute-start | bytes 1228808 | tf_op jit(solution)/shard_map/ppermute | solution.py:31
  100.0 17.6 %collective-permute-start.14 = (bf16[320,640]{1,0:T(8,128)(2,1)}, bf16[320,640]{1,0:T(8,128)(2,1)}, u32[]{:S(2)}, u32[]{:S(2)}) collective-permute-start(bf16[320,640]{1,0:T(8,128)(2,1)} %collective-permute-done.13.refs_6_), channel_id=1, source_target_pairs={{0,1},{1,2},{2,3},{3,4},{4,5},{5,6},{6,7},{7,0},{8,9},{9,10},{10,1... | collective-permute-start | bytes 1228808 | tf_op jit(solution)/shard_map/ppermute | solution.py:31
  100.0 17.6 %copy-start.5 = (bf16[328,896]{1,0:T(8,128)(2,1)}, bf16[328,896]{1,0:T(8,128)(2,1)S(1)}, u32[]{:S(2)}) copy-start(bf16[328,896]{1,0:T(8,128)(2,1)S(1)} %collective-permute-done.6.refs_10_.refs_3_) | copy-start | bytes 1763332
  100.0 17.8 %collective-permute-start.8 = (bf16[328,896]{1,0:T(8,128)(2,1)S(1)}, bf16[328,896]{1,0:T(8,128)(2,1)S(1)}, u32[]{:S(2)}, u32[]{:S(2)}) collective-permute-start(bf16[328,896]{1,0:T(8,128)(2,1)S(1)} %collective-permute-done.6.refs_10_.refs_3_), channel_id=1, source_target_pairs={{0,8},{8,0},{16,24},{24,16},{32,40},{40,32},{48,56},{56,48},{64,72... | collective-permute-start | bytes 1763336 | tf_op jit(solution)/shard_map/ppermute | solution.py:44
  106.4 11.3 %collective-permute-start.18 = (bf16[320,640]{1,0:T(8,128)(2,1)}, bf16[320,640]{1,0:T(8,128)(2,1)}, u32[]{:S(2)}, u32[]{:S(2)}) collective-permute-start(bf16[320,640]{1,0:T(8,128)(2,1)} %collective-permute-done.17.refs_2_), channel_id=1, source_target_pairs={{0,7},{1,0},{2,1},{3,2},{4,3},{5,4},{6,5},{7,6},{8,15},{9,8},{10,9... | collective-permute-start | bytes 1228808 | tf_op jit(solution)/shard_map/ppermute | solution.py:32
  111.7 5.9 %copy-start.8 = (bf16[328,896]{1,0:T(8,128)(2,1)S(1)}, bf16[328,896]{1,0:T(8,128)(2,1)}, u32[]{:S(2)}) copy-start(bf16[328,896]{1,0:T(8,128)(2,1)} %copy-done.7) | copy-start | bytes 1763332
  111.7 5.9 %copy-start.10 = (bf16[328,896]{1,0:T(8,128)(2,1)S(1)}, bf16[328,896]{1,0:T(8,128)(2,1)}, u32[]{:S(2)}) copy-start(bf16[328,896]{1,0:T(8,128)(2,1)} %copy-done.9) | copy-start | bytes 1763332
  111.7 5.9 %copy-start.12 = (bf16[328,896]{1,0:T(8,128)(2,1)S(1)}, bf16[328,896]{1,0:T(8,128)(2,1)}, u32[]{:S(2)}) copy-start(bf16[328,896]{1,0:T(8,128)(2,1)} %copy-done.11) | copy-start | bytes 1763332
  115.6 10.3 %collective-permute-start.11 = (bf16[320,640]{1,0:T(8,128)(2,1)}, bf16[320,640]{1,0:T(8,128)(2,1)}, u32[]{:S(2)}, u32[]{:S(2)}) collective-permute-start(bf16[320,640]{1,0:T(8,128)(2,1)} %collective-permute-done.10.refs_2_), channel_id=1, source_target_pairs={{0,7},{1,0},{2,1},{3,2},{4,3},{5,4},{6,5},{7,6},{8,15},{9,8},{10,9... | collective-permute-start | bytes 1228808 | tf_op jit(solution)/shard_map/ppermute | solution.py:32
  117.6 10.4 %collective-permute-start.15 = (bf16[320,640]{1,0:T(8,128)(2,1)}, bf16[320,640]{1,0:T(8,128)(2,1)}, u32[]{:S(2)}, u32[]{:S(2)}) collective-permute-start(bf16[320,640]{1,0:T(8,128)(2,1)} %collective-permute-done.14.refs_5_), channel_id=1, source_target_pairs={{0,1},{1,2},{2,3},{3,4},{4,5},{5,6},{6,7},{7,0},{8,9},{9,10},{10,1... | collective-permute-start | bytes 1228808 | tf_op jit(solution)/shard_map/ppermute | solution.py:36
  117.7 21.8 %collective-permute-start.22 = (bf16[320,640]{1,0:T(8,128)(2,1)}, bf16[320,640]{1,0:T(8,128)(2,1)S(1)}, u32[]{:S(2)}, u32[]{:S(2)}) collective-permute-start(bf16[320,640]{1,0:T(8,128)(2,1)} %collective-permute-done.21.refs_6_), channel_id=1, source_target_pairs={{0,1},{1,2},{2,3},{3,4},{4,5},{5,6},{6,7},{7,0},{8,9},{9,10},{10,1... | collective-permute-start | bytes 1228808 | tf_op jit(solution)/shard_map/ppermute | solution.py:31
  117.8 10.1 %copy-start.6 = (bf16[328,896]{1,0:T(8,128)(2,1)}, bf16[328,896]{1,0:T(8,128)(2,1)S(1)}, u32[]{:S(2)}) copy-start(bf16[328,896]{1,0:T(8,128)(2,1)S(1)} %collective-permute-done.8.refs_11_.refs_4_) | copy-start | bytes 1763332
  117.8 21.7 %collective-permute-start.19 = (bf16[320,640]{1,0:T(8,128)(2,1)}, bf16[320,640]{1,0:T(8,128)(2,1)S(1)}, u32[]{:S(2)}, u32[]{:S(2)}) collective-permute-start(bf16[320,640]{1,0:T(8,128)(2,1)} %collective-permute-done.18.refs_3_), channel_id=1, source_target_pairs={{0,7},{1,0},{2,1},{3,2},{4,3},{5,4},{6,5},{7,6},{8,15},{9,8},{10,9... | collective-permute-start | bytes 1228808 | tf_op jit(solution)/shard_map/ppermute | solution.py:38
  148.7 39.1 %copy-start.1 = (bf16[640,256]{1,0:T(8,128)(2,1)S(1)}, bf16[640,256]{1,0:T(8,128)(2,1)}, u32[]{:S(2)}) copy-start(bf16[640,256]{1,0:T(8,128)(2,1)} %get-tuple-element.13.own) | copy-start | bytes 983044
  148.7 41.1 %copy-start.20 = (s32[8]{0:T(128)S(1)}, s32[8]{0:T(128)}, u32[]{:S(2)}) copy-start(s32[8]{0:T(128)} %param.13) | copy-start | bytes 100
  148.7 6.5 %collective-permute-start.25 = (bf16[640,256]{1,0:T(8,128)(2,1)}, bf16[640,256]{1,0:T(8,128)(2,1)S(1)}, u32[]{:S(2)}, u32[]{:S(2)}) collective-permute-start(bf16[640,256]{1,0:T(8,128)(2,1)} %get-tuple-element.13.own), channel_id=1, source_target_pairs={{0,112},{8,120},{16,0},{24,8},{32,16},{40,24},{48,32},{56,40},{64,... | collective-permute-start | bytes 983048 | tf_op jit(solution)/shard_map/ppermute | solution.py:32
  149.7 7.3 %collective-permute-start.23 = (bf16[640,256]{1,0:T(8,128)(2,1)}, bf16[640,256]{1,0:T(8,128)(2,1)S(1)}, u32[]{:S(2)}, u32[]{:S(2)}) collective-permute-start(bf16[640,256]{1,0:T(8,128)(2,1)} %get-tuple-element.13.own), channel_id=1, source_target_pairs={{0,16},{8,24},{16,32},{24,40},{32,48},{40,56},{48,64},{56,72},{64,... | collective-permute-start | bytes 983048 | tf_op jit(solution)/shard_map/ppermute | solution.py:31
  155.2 9.5 %collective-permute-start.26 = (bf16[640,256]{1,0:T(8,128)(2,1)S(1)}, bf16[640,256]{1,0:T(8,128)(2,1)S(1)}, u32[]{:S(2)}, u32[]{:S(2)}) collective-permute-start(bf16[640,256]{1,0:T(8,128)(2,1)S(1)} %collective-permute-done.25), channel_id=1, source_target_pairs={{0,112},{8,120},{16,0},{24,8},{32,16},{40,24},{48,32},{56,40},{64,... | collective-permute-start | bytes 983048 | tf_op jit(solution)/shard_map/ppermute | solution.py:32
  157.1 10.5 %collective-permute-start.28 = (bf16[640,256]{1,0:T(8,128)(2,1)S(1)}, bf16[640,256]{1,0:T(8,128)(2,1)S(1)}, u32[]{:S(2)}, u32[]{:S(2)}) collective-permute-start(bf16[640,256]{1,0:T(8,128)(2,1)S(1)} %collective-permute-done.23.far), channel_id=1, source_target_pairs={{0,16},{8,24},{16,32},{24,40},{32,48},{40,56},{48,64},{56,72},{64,... | collective-permute-start | bytes 983048 | tf_op jit(solution)/shard_map/ppermute | solution.py:31
  164.7 9.4 %collective-permute-start.27 = (bf16[640,256]{1,0:T(8,128)(2,1)S(1)}, bf16[640,256]{1,0:T(8,128)(2,1)S(1)}, u32[]{:S(2)}, u32[]{:S(2)}) collective-permute-start(bf16[640,256]{1,0:T(8,128)(2,1)S(1)} %collective-permute-done.26), channel_id=1, source_target_pairs={{0,112},{8,120},{16,0},{24,8},{32,16},{40,24},{48,32},{56,40},{64,... | collective-permute-start | bytes 983048 | tf_op jit(solution)/shard_map/ppermute | solution.py:32
  167.6 10.2 %collective-permute-start.29 = (bf16[640,256]{1,0:T(8,128)(2,1)S(1)}, bf16[640,256]{1,0:T(8,128)(2,1)S(1)}, u32[]{:S(2)}, u32[]{:S(2)}) collective-permute-start(bf16[640,256]{1,0:T(8,128)(2,1)S(1)} %collective-permute-done.28), channel_id=1, source_target_pairs={{0,16},{8,24},{16,32},{24,40},{32,48},{40,56},{48,64},{56,72},{64,... | collective-permute-start | bytes 983048 | tf_op jit(solution)/shard_map/ppermute | solution.py:31
  177.9 40.8 %collective-permute-start.30 = (bf16[4480,256]{1,0:T(8,128)(2,1)S(1)}, bf16[4480,256]{1,0:T(8,128)(2,1)}, u32[]{:S(2)}, u32[]{:S(2)}) collective-permute-start(bf16[4480,256]{1,0:T(8,128)(2,1)S(1)} %constant_dynamic-update-slice_fusion.7.mine), channel_id=1, source_target_pairs={{0,8},{8,0},{16,24},{24,16},{32,40},{40,32},{48,56},{56,48},{64,72... | collective-permute-start | bytes 6881288 | tf_op jit(solution)/shard_map/ppermute | solution.py:44
  187.8 10.9 %collective-permute-start.24 = (bf16[640,256]{1,0:T(8,128)(2,1)S(1)}, bf16[640,256]{1,0:T(8,128)(2,1)S(1)}, u32[]{:S(2)}, u32[]{:S(2)}) collective-permute-start(bf16[640,256]{1,0:T(8,128)(2,1)S(1)} %copy-done.1), channel_id=1, source_target_pairs={{0,8},{8,16},{16,24},{24,32},{32,40},{40,48},{48,56},{56,64},{64,7... | collective-permute-start | bytes 983048 | tf_op jit(solution)/shard_map/ppermute | solution.py:466
  189.9 8.9 %copy-start.4 = (bf16[5,320,128]{2,1,0:T(8,128)(2,1)S(1)}, bf16[5,320,128]{2,1,0:T(8,128)(2,1)}, u32[]{:S(2)}) copy-start(bf16[5,320,128]{2,1,0:T(8,128)(2,1)} %get-tuple-element.10.q_a) | copy-start | bytes 1228804
  198.6 9.1 %collective-permute-start.31 = (bf16[640,256]{1,0:T(8,128)(2,1)}, bf16[640,256]{1,0:T(8,128)(2,1)S(1)}, u32[]{:S(2)}, u32[]{:S(2)}) collective-permute-start(bf16[640,256]{1,0:T(8,128)(2,1)} %copy-done.17), channel_id=1, source_target_pairs={{0,112},{8,120},{16,0},{24,8},{32,16},{40,24},{48,32},{56,40},{64,... | collective-permute-start | bytes 983048 | tf_op jit(solution)/shard_map/ppermute | solution.py:38
  207.7 11.0 %collective-permute-start.32 = (bf16[640,256]{1,0:T(8,128)(2,1)S(1)}, bf16[640,256]{1,0:T(8,128)(2,1)S(1)}, u32[]{:S(2)}, u32[]{:S(2)}) collective-permute-start(bf16[640,256]{1,0:T(8,128)(2,1)S(1)} %collective-permute-done.31.mine_mid), channel_id=1, source_target_pairs={{0,8},{8,0},{16,24},{24,16},{32,40},{40,32},{48,56},{56,48},{64,72... | collective-permute-start | bytes 983048 | tf_op jit(solution)/shard_map/ppermute | solution.py:44
  (6 other events, 11.8 us)

commit v2 on v1

v2 whole, which is shorter than its diff:
```python
import functools
import math

import jax
import jax.numpy as jnp
from jax import lax
from jax.experimental import pallas as pl
from jax.experimental.pallas import tpu as pltpu
from jax.sharding import PartitionSpec as P


HD = 128
BLOCK = 128
LEN_BLOCKS = 11
EPSILON = 1e-06
THETA = 1000000.0
VMEM = pltpu.MemorySpace.VMEM
SMEM = pltpu.MemorySpace.SMEM
MIB = 1024 * 1024


def ring(block, axis, hop, last_ahead, tied=None):
    size = lax.axis_size(axis)
    count = size // hop
    ahead = [(i, (i + hop) % size) for i in range(size)]
    back = [(i, (i - hop) % size) for i in range(size)]
    got = {0: block}
    up = down = block
    for step in range(1, count // 2):
        up = lax.ppermute(up, axis, ahead)
        down = lax.ppermute(down, axis, back)
        got[count - step] = up
        got[step] = down
        if tied and step == 1:
            up, *tied[:] = lax.optimization_barrier((up, *tied))
    if last_ahead:
        got[count // 2] = lax.ppermute(up, axis, ahead)
    else:
        got[count // 2] = lax.ppermute(down, axis, back)
    return [got[i] for i in range(count)]


def swap(block, axis):
    size = lax.axis_size(axis)
    return lax.ppermute(block, axis, [(i, i ^ 1) for i in range(size)])


def by_arrival(count):
    order = [0]
    for step in range(1, count // 2):
        order += [step, count - step]
    return order


def weight_copies(place, weights, wbuf, sem, count, feat, lo, width):
    tp, chip, core = place[0], place[1], place[2]
    mine, other, mine_mid, other_mid = weights
    w_rows = feat // 2
    copies = []
    for k, rel in enumerate([*by_arrival(count), count // 2]):
        i = jnp.bitwise_and(chip + rel - tp, count - 1)
        for which in range(2):
            spot = core if which == 0 else 1 - core
            if rel == count // 2:
                src = mine_mid if which == 0 else other_mid
            else:
                src = (mine if which == 0 else other).at[k]
            copies.append(
                pltpu.make_async_copy(
                    src.at[pl.ds(0, w_rows), pl.ds(lo, width)],
                    wbuf.at[pl.ds(pl.multiple_of(i * feat + spot * w_rows, 64), w_rows)],
                    sem.at[2 * rel + which],
                )
            )
    return copies


def rotated(head, cos, sin):
    return (head * cos[...] + pltpu.roll(head, HD // 2, 1) * sin[...]).astype(jnp.bfloat16)


def keys_kernel(place, *refs, count, part, feat, lo):
    pieces = refs[: 2 * count]
    weights = refs[2 * count : 2 * count + 4]
    gain, cos, sin, kv, labels, normed = refs[2 * count + 4 : 2 * count + 10]
    xbuf, wbuf, acc, tags, sem_x, sem_w, sem_tag, sem_out = refs[2 * count + 10 :]
    w_rows = feat // 2
    tile = 64
    mid = count // 2

    def x_copy(half, i):
        return pltpu.make_async_copy(
            pieces[half * count + i],
            xbuf.at[pl.ds(half * part, part), pl.ds(i * feat, feat)],
            sem_x.at[half * count + i],
        )

    def tag_copies():
        copies = []
        for which in range(2):
            for k, rel in enumerate([*by_arrival(count), mid]):
                src = weights[2 + which] if rel == mid else weights[which].at[k]
                copies.append(
                    pltpu.make_async_copy(
                        src.at[pl.ds(w_rows, 8), pl.ds(0, 128)],
                        tags.at[which * count + rel],
                        sem_tag.at[which * count + rel],
                    )
                )
        return copies

    w_copies = weight_copies(place, weights, wbuf, sem_w, count, feat, lo, 2 * HD)
    t_copies = tag_copies()
    for i in range(count):
        x_copy(0, i).start()
    for i in range(count):
        x_copy(1, i).start()
    for copy in w_copies + t_copies:
        copy.start()

    def normalize(r, unused):
        at_rows = pl.ds(pl.multiple_of(r * tile, tile), tile)
        totals = [jnp.zeros((tile, 128), jnp.float32) for _ in range(2)]
        for g in range(count * feat // 128):
            part_x = xbuf[at_rows, g * 128 : (g + 1) * 128].astype(jnp.float32)
            totals[g % 2] = totals[g % 2] + part_x * part_x
        mean = jnp.sum(totals[0] + totals[1], axis=1, keepdims=True) * (1.0 / (feat * count))
        scale = jnp.broadcast_to(lax.rsqrt(mean + EPSILON), (tile, 128))
        for g in range(count * feat // 128):
            at_col = slice(g * 128, (g + 1) * 128)
            part_x = xbuf[at_rows, at_col].astype(jnp.float32)
            xbuf[at_rows, at_col] = (part_x * scale * gain[:, at_col]).astype(jnp.bfloat16)
        return unused

    handed = []
    for half in range(2):
        for i in range(count):
            x_copy(half, i).wait()
        lax.fori_loop(half * part // tile, (half + 1) * part // tile, normalize, 0)
        rows = pl.ds(half * part, part)
        handed.append(pltpu.make_async_copy(xbuf.at[rows], normed.at[rows], sem_out.at[half]))
        handed[-1].start()
    for copy in w_copies:
        copy.wait()
    acc[...] = jnp.dot(xbuf[...], wbuf[...], preferred_element_type=jnp.float32)
    kv[:, :HD] = rotated(acc[:, :HD], cos, sin)
    kv[:, HD:] = acc[:, HD:].astype(jnp.bfloat16)
    for copy in t_copies:
        copy.wait()
    for r in range(2 * count):
        labels[r : r + 1, :] = tags[r].astype(jnp.float32)[0:1].astype(jnp.int32)
    for copy in handed:
        copy.wait()


def queries_kernel(place, x, mine, other, mine_mid, other_mid, cos, sin, q, xbuf, wbuf, acc, sem_x, sem_w, *, count, part, feat, heads):
    def x_copy(half):
        rows = pl.ds(half * part, part)
        return pltpu.make_async_copy(x.at[rows], xbuf.at[rows], sem_x.at[half])

    weights = (mine, other, mine_mid, other_mid)
    w_copies = weight_copies(place, weights, wbuf, sem_w, count, feat, 0, heads * HD)
    for copy in w_copies:
        copy.start()
    for half in range(2):
        x_copy(half).start()
    for copy in w_copies:
        copy.wait()

    def one_half(half, unused):
        x_copy(half).wait()
        rows = pl.ds(pl.multiple_of(half * part, 64), part)
        acc[...] = jnp.dot(xbuf[rows], wbuf[...], preferred_element_type=jnp.float32)
        for h in range(heads):
            q[h, rows] = rotated(acc[:, h * HD : (h + 1) * HD], cos.at[rows], sin.at[rows])
        return unused

    lax.fori_loop(0, 2, one_half, 0)


def project_keys(place, pieces, weights, gain, cos, sin, lo):
    count = len(pieces) // 2
    part, feat = pieces[0].shape
    tok = 2 * part
    return pl.pallas_call(
        functools.partial(keys_kernel, count=count, part=part, feat=feat, lo=lo),
        out_shape=(
            jax.ShapeDtypeStruct((tok, 2 * HD), jnp.bfloat16),
            jax.ShapeDtypeStruct((2 * count, 128), jnp.int32),
            jax.ShapeDtypeStruct((tok, count * feat), jnp.bfloat16),
        ),
        in_specs=[pl.BlockSpec(memory_space=SMEM)]
        + [pl.BlockSpec(memory_space=pl.ANY)] * (len(pieces) + 4)
        + [pl.BlockSpec(memory_space=VMEM)] * 3,
        out_specs=(
            pl.BlockSpec(memory_space=VMEM),
            pl.BlockSpec(memory_space=VMEM),
            pl.BlockSpec(memory_space=pl.ANY),
        ),
        scratch_shapes=[
            pltpu.VMEM((tok, count * feat), jnp.bfloat16),
            pltpu.VMEM((count * feat, 2 * HD), jnp.bfloat16),
            pltpu.VMEM((tok, 2 * HD), jnp.float32),
            pltpu.VMEM((2 * count, 8, 128), jnp.bfloat16),
            pltpu.SemaphoreType.DMA((2 * count,)),
            pltpu.SemaphoreType.DMA((2 * count,)),
            pltpu.SemaphoreType.DMA((2 * count,)),
            pltpu.SemaphoreType.DMA((2,)),
        ],
        compiler_params=pltpu.CompilerParams(vmem_limit_bytes=16 * MIB),
        cost_estimate=pl.CostEstimate(
            flops=4 * tok * feat * count * HD, bytes_accessed=4 * tok * feat * count, transcendentals=0
        ),
    )(place, *pieces, *weights, gain, cos, sin)


def project_queries(place, normed, weights, cos, sin, heads):
    count = weights[0].shape[0] + 1
    tok = normed.shape[0]
    part = tok // 2
    feat = normed.shape[1] // count
    width = heads * HD
    return pl.pallas_call(
        functools.partial(queries_kernel, count=count, part=part, feat=feat, heads=heads),
        out_shape=jax.ShapeDtypeStruct((heads, tok, HD), jnp.bfloat16),
        in_specs=[pl.BlockSpec(memory_space=SMEM)]
        + [pl.BlockSpec(memory_space=pl.ANY)] * 5
        + [pl.BlockSpec(memory_space=VMEM)] * 2,
        out_specs=pl.BlockSpec(memory_space=VMEM),
        scratch_shapes=[
            pltpu.VMEM((tok, count * feat), jnp.bfloat16),
            pltpu.VMEM((count * feat, width), jnp.bfloat16),
            pltpu.VMEM((part, width), jnp.float32),
            pltpu.SemaphoreType.DMA((2,)),
            pltpu.SemaphoreType.DMA((2 * count,)),
        ],
        compiler_params=pltpu.CompilerParams(vmem_limit_bytes=20 * MIB),
        cost_estimate=pl.CostEstimate(
            flops=2 * tok * feat * count * width, bytes_accessed=2 * tok * feat * count, transcendentals=0
        ),
    )(place, normed, *weights, cos, sin)


def attend_kernel(
    info, q_in, far, near, own, *refs, lo, hi
):
    out, qbuf, kvbuf, sbuf, mbuf, lbuf, obuf, tbuf, sems, sem_out = refs[-10:]
    heads = q_in.shape[0]
    tok = own.shape[0]
    local = tok // BLOCK
    back = 2 * local
    span_in = pl.ds(lo * BLOCK, (hi - lo) * BLOCK)
    copies = [
        pltpu.make_async_copy(q_in.at[:, span_in], qbuf.at[:, span_in], sems.at[0]),
        pltpu.make_async_copy(far, kvbuf.at[pl.ds(BLOCK, tok)], sems.at[1]),
        pltpu.make_async_copy(near, kvbuf.at[pl.ds(BLOCK + tok, tok)], sems.at[2]),
        pltpu.make_async_copy(own, kvbuf.at[pl.ds(BLOCK + 2 * tok, tok)], sems.at[3]),
    ]
    for copy in copies:
        copy.start()
    kvbuf[:BLOCK] = jnp.zeros((BLOCK, 2 * HD), jnp.bfloat16)
    for copy in copies:
        copy.wait()
    first = info[0]
    n_prompts = info.shape[0] - 1
    factor = math.log2(math.e) / math.sqrt(HD)
    rows = heads * BLOCK
    row = lax.broadcasted_iota(jnp.int32, (BLOCK, BLOCK), 0)
    col = lax.broadcasted_iota(jnp.int32, (BLOCK, BLOCK), 1)
    causal = col <= row

    def result_copy(i):
        at = pl.ds(pl.multiple_of(i * BLOCK, BLOCK), BLOCK)
        return pltpu.make_async_copy(tbuf.at[i - lo], out.at[at], sem_out.at[i - lo])

    def one_block(i, unused):
        block = first + i

        def find(p, state):
            start, best = state
            best = jnp.where(start <= block, start, best)
            return start + info[1 + p], best

        _, begin = lax.fori_loop(0, n_prompts, find, (jnp.int32(0), jnp.int32(0)))
        low = jnp.maximum(begin - first + back, i) + 1
        last = back + i + 1
        pairs = (last - low + 2) // 2
        q = qbuf[:, pl.ds(pl.multiple_of(i * BLOCK, BLOCK), BLOCK), :].reshape(rows, HD)

        def span(t):
            return pl.ds(pl.multiple_of((last - 1 - 2 * t) * BLOCK, BLOCK), 2 * BLOCK)

        def score(t, h):
            s = lax.dot_general(
                q[h * BLOCK : (h + 1) * BLOCK],
                kvbuf[span(t), :HD],
                (((1,), (1,)), ((), ())),
                preferred_element_type=jnp.float32,
            )
            inside = last - 1 - 2 * t >= low
            bias = jnp.where(inside, 0.0, -1e30)
            return s[:, :BLOCK] * factor + bias, s[:, BLOCK:] * factor

        mbuf[...] = jnp.full_like(mbuf, -1e30)

        def upward(t, unused):
            shut = jnp.where(t == 0, -1e30, 0.0)
            for h in range(heads):
                at = slice(h * BLOCK, (h + 1) * BLOCK)
                left, right = score(t, h)
                right = right + jnp.where(causal, 0.0, shut)
                sbuf[t, at, :BLOCK] = left
                sbuf[t, at, BLOCK:] = right
                mbuf[at] = jnp.maximum(mbuf[at], jnp.maximum(left, right))
            return unused

        lax.fori_loop(0, pairs, upward, 0)
        top = jnp.max(mbuf[...], axis=1, keepdims=True)
        mbuf[...] = jnp.broadcast_to(top, mbuf.shape)
        lbuf[...] = jnp.zeros_like(lbuf)
        obuf[...] = jnp.zeros_like(obuf)

        def gather(t, unused):
            for h in range(heads):
                at = slice(h * BLOCK, (h + 1) * BLOCK)
                peak = mbuf[at]
                left = jnp.exp2(sbuf[t, at, :BLOCK] - peak)
                right = jnp.exp2(sbuf[t, at, BLOCK:] - peak)
                lbuf[at] += left + right
                p = jnp.concatenate([left.astype(jnp.bfloat16), right.astype(jnp.bfloat16)], axis=1)
                obuf[at] += jnp.dot(p, kvbuf[span(t), HD:], preferred_element_type=jnp.float32)
            return unused

        lax.fori_loop(0, pairs, gather, 0)
        total = jnp.sum(lbuf[...], axis=1, keepdims=True)
        result = (obuf[...] / total).astype(jnp.bfloat16)
        for h in range(heads):
            tbuf[i - lo, :, h * HD : (h + 1) * HD] = result[h * BLOCK : (h + 1) * BLOCK]
        result_copy(i).start()
        return unused

    lax.fori_loop(lo, hi, one_block, 0)
    for i in range(lo, hi):
        result_copy(i).wait()


def attend(info, q, far, near, own, lo, hi, base=None):
    heads = q.shape[0]
    tok = own.shape[0]
    operands = [info, q, far, near, own]
    if base is not None:
        operands.append(base)
    return pl.pallas_call(
        functools.partial(attend_kernel, lo=lo, hi=hi),
        out_shape=jax.ShapeDtypeStruct((tok, heads * HD), jnp.bfloat16),
        in_specs=[pl.BlockSpec(memory_space=SMEM)]
        + [pl.BlockSpec(memory_space=pl.ANY)] * (len(operands) - 1),
        out_specs=pl.BlockSpec(memory_space=pl.ANY),
        scratch_shapes=[
            pltpu.VMEM((heads, tok, HD), jnp.bfloat16),
            pltpu.VMEM((3 * tok + BLOCK, 2 * HD), jnp.bfloat16),
            pltpu.VMEM(((LEN_BLOCKS + 1) // 2, heads * BLOCK, 2 * BLOCK), jnp.float32),
            pltpu.VMEM((heads * BLOCK, BLOCK), jnp.float32),
            pltpu.VMEM((heads * BLOCK, BLOCK), jnp.float32),
            pltpu.VMEM((heads * BLOCK, HD), jnp.float32),
            pltpu.VMEM((hi - lo, BLOCK, heads * HD), jnp.bfloat16),
            pltpu.SemaphoreType.DMA((4,)),
            pltpu.SemaphoreType.DMA((hi - lo,)),
        ],
        input_output_aliases={5: 0} if base is not None else {},
        compiler_params=pltpu.CompilerParams(vmem_limit_bytes=12 * MIB),
        cost_estimate=pl.CostEstimate(
            flops=2 * 10**9 * (hi - lo), bytes_accessed=4 * 10**6, transcendentals=10**6
        ),
    )(*operands)


def cache_kernel(place, labels, table, mine, other, mine_mid, other_mid, out, sem, *, local, count, tok):
    chip, core, me = place[1], place[2], place[3]
    mid = count // 2
    slots = out.shape[0]

    def put(src, at_row, slot):
        return pltpu.make_async_copy(src.at[pl.ds(pl.multiple_of(at_row, BLOCK), BLOCK)], out.at[slot], sem)

    def one(source, rank):
        rel = jnp.bitwise_and(jnp.right_shift(source, 1) - chip, count - 1)
        same = jnp.bitwise_and(source, 1) == core
        middle = rel == mid
        spot = jnp.where(rel > mid, 2 * (count - rel), jnp.where(middle, 0, jnp.maximum(2 * rel - 1, 0)))
        label_row = jnp.where(same, rel, count + rel)
        for inner in range(local):
            hit = labels[label_row, inner] == me

            @pl.when(hit)
            def _():
                slot = table[0, rank]
                at_row = spot * tok + inner * BLOCK

                @pl.when(same & jnp.logical_not(middle))
                def _():
                    put(mine, at_row, slot).start()

                @pl.when(jnp.logical_not(same) & jnp.logical_not(middle))
                def _():
                    put(other, at_row, slot).start()

                @pl.when(same & middle)
                def _():
                    put(mine_mid, at_row, slot).start()

                @pl.when(jnp.logical_not(same) & middle)
                def _():
                    put(other_mid, at_row, slot).start()

            rank = rank + hit.astype(jnp.int32)
        return rank

    found = lax.fori_loop(0, 2 * count, one, jnp.int32(0))

    def clear(r, unused):
        out[table[0, r]] = jnp.zeros(out.shape[1:], out.dtype)
        return unused

    lax.fori_loop(found, slots, clear, 0)

    def settle(r, unused):
        put(mine, 0, 0).wait()
        return unused

    lax.fori_loop(0, found, settle, 0)


def fill_cache(place, labels, table, mine, other, mine_mid, other_mid, local, count):
    tok = mine_mid.shape[0]
    slots = table.shape[1]
    return pl.pallas_call(
        functools.partial(cache_kernel, local=local, count=count, tok=tok),
        out_shape=jax.ShapeDtypeStruct((slots, BLOCK, mine.shape[1]), jnp.bfloat16),
        in_specs=[pl.BlockSpec(memory_space=SMEM)] * 3 + [pl.BlockSpec(memory_space=pl.ANY)] * 4,
        out_specs=pl.BlockSpec(memory_space=VMEM),
        scratch_shapes=[pltpu.SemaphoreType.DMA],
        compiler_params=pltpu.CompilerParams(vmem_limit_bytes=8 * MIB),
    )(place, labels, table, mine, other, mine_mid, other_mid)


def on_device(
    hidden_states, norm_gain, w_query, w_key, w_value, prompt_blocks, owner_map, slot_table
):
    tok, feat = hidden_states.shape
    n_dev = lax.axis_size("dev")
    n_tp = lax.axis_size("tp")
    device = lax.axis_index("dev")
    count = n_dev // 2
    assert count & (count - 1) == 0 and count == n_tp
    mid = count // 2
    local = tok // BLOCK
    heads = w_query.shape[1] // HD
    place = jnp.stack([lax.axis_index("tp"), device // 2, device % 2, device]).astype(jnp.int32)

    token_rows = device * tok + jnp.arange(tok, dtype=jnp.int32)
    starts = (jnp.cumsum(prompt_blocks) - prompt_blocks) * BLOCK
    start_of = jnp.max(jnp.where(token_rows[:, None] >= starts[None, :], starts[None, :], 0), axis=1)
    offsets = token_rows - start_of
    freq_index = jnp.arange(HD // 2, dtype=jnp.float32)
    inverse = jnp.exp(freq_index * (-2.0 * math.log(THETA) / HD))
    angles = offsets.astype(jnp.float32)[:, None] * inverse[None, :]
    cosine, sine = jnp.cos(angles), jnp.sin(angles)
    cos = jnp.concatenate([cosine, cosine], axis=1)
    sin = jnp.concatenate([-sine, sine], axis=1)
    gain = norm_gain.astype(jnp.float32)
    gain = lax.dynamic_slice_in_dim(
        jnp.concatenate([gain, gain]), lax.axis_index("tp") * feat, n_tp * feat
    )[None]
    info = jnp.concatenate([(device * local)[None].astype(jnp.int32), prompt_blocks])

    part = tok // 2
    tied = [cos, sin, gain, place, info]
    x_a = ring(hidden_states[:part], "tp", 1, True)
    x_b = ring(hidden_states[part:], "tp", 1, False, tied)
    cos, sin, gain, place, info = tied

    weights = jnp.concatenate([w_query, w_key, w_value], axis=1)
    w_cols = weights.shape[1]
    labels = jnp.pad(owner_map.astype(jnp.bfloat16)[None], ((0, 7), (0, w_cols - local)))
    weights = jnp.concatenate([weights, labels], axis=0)
    arrival = by_arrival(count)
    w_got = ring(weights, "dev", 2, True)
    w_mine = jnp.stack([w_got[i] for i in arrival])
    w_other = swap(w_mine, "dev")
    w_other_mid = swap(w_got[mid], "dev")
    w_set = (w_mine, w_other, w_got[mid], w_other_mid)

    kv, labels, normed = project_keys(place, [*x_a, *x_b], w_set, gain, cos, sin, heads * HD)
    q = project_queries(place, normed, w_set, cos, sin, heads)

    near = lax.ppermute(kv, "dev", [(i, i + 1) for i in range(n_dev - 1)])
    k_got = ring(kv, "dev", 2, False)
    far = k_got[count - 1]
    cuts = (0, local // 2, local - 1, local)
    context = attend(info, q, far, near, kv, cuts[0], cuts[1])
    context = attend(info, q, far, near, kv, cuts[1], cuts[2], base=context)
    context = attend(info, q, far, near, kv, cuts[2], cuts[3], base=context)
    k_mine = jnp.concatenate([k_got[i] for i in arrival], axis=0)
    k_other = swap(k_mine, "dev")
    k_mid_other = swap(k_got[mid], "dev")
    kv_cache = fill_cache(
        place, labels, slot_table, k_mine, k_other, k_got[mid], k_mid_other, local, count
    )
    return (context, kv_cache)


def solution(mesh):
    in_specs = (
        P(("groups", "dev"), "tp"),
        P(),
        P("dev", "tp"),
        P("dev", "tp"),
        P("dev", "tp"),
        P("groups"),
        P(("groups", "dev")),
        P(("groups", "dev"), None),
    )
    out_specs = (P(("groups", "dev"), "tp"), P(("groups", "dev"), None, "tp"))

    return jax.shard_map(on_device, mesh=mesh, in_specs=in_specs, out_specs=out_specs, check_vma=False)
```

time: 223 us -> 208 us (0.933); the launches traced: 222 us -> 205 us
  waiting for transfers between devices: 85.5 us -> 98.6 us
  Pallas kernels: 47.3 us -> 35.5 us
  local copies, waits for them, and re-layouts: 14.9 us -> 5.49 us
  starting transfers between devices: 63.7 us -> 58.3 us
  other arithmetic: 9.44 us -> 5.81 us
    ppermute x12, waiting for transfers between devices: 14.6 us -> 28.4 us  [ring(): up = lax.ppermute(up, axis, ahead)]
    pallas_call x3 -> x2, Pallas kernels: 28.5 us -> 16.8 us  [the longest x1 8.97 us: project_queries(): pl.pallas_call(functools.partial(queries_kernel, count=count, part=part,...]
    ppermute x12, waiting for transfers between devices: 66.9 us -> 55.7 us  [ring(): down = lax.ppermute(down, axis, back)]
    ppermute x2, waiting for transfers between devices: 2.06 us -> 11.6 us  [ring(): got[count // 2] = lax.ppermute(up, axis, ahead)]
    unnamed x58 -> x19, local copies, waits for them, and re-layouts: 9.04 us -> 4.47 us
    ppermute x4, starting transfers between devices: 23.8 us -> 19.3 us  [swap(): return lax.ppermute(block, axis, [(i, i ^ 1) for i in range(size)])]
  transfers between devices with their start and end apart: 33 -> 33, of which waited for: 20 -> 21; matrix products, arithmetic and copies ran while one was open for 8% -> 4% of each run, Pallas kernels for 16% -> 12%
where the time goes in v2:
time: 208 us; the launch traced here: 205 us
  waiting for transfers between devices  98.6 us (47%)
  starting transfers between devices  58.3 us (28%)
  Pallas kernels  35.5 us (17%)
  other arithmetic  5.81 us (3%)
  local copies, waits for them, and re-layouts  5.49 us (3%)
    ppermute x12, waiting for transfers between devices, ring(): down = lax.ppermute(down, axis, back)  55.7 us
    ppermute x12, starting transfers between devices, ring(): down = lax.ppermute(down, axis, back)  31.3 us
    ppermute x12, waiting for transfers between devices, ring(): up = lax.ppermute(up, axis, ahead)  28.4 us
    ppermute x4, starting transfers between devices, swap(): return lax.ppermute(block, axis, [(i, i ^ 1) for i in range(size)])  19.3 us
    pallas_call x3, Pallas kernels, attend(): pl.pallas_call(functools.partial(attend_kernel, lo=lo, hi=hi), out_shape=...  15.4 us
    ppermute x2, waiting for transfers between devices, ring(): got[count // 2] = lax.ppermute(up, axis, ahead)  11.6 us
    pallas_call x1, Pallas kernels, project_queries(): pl.pallas_call(functools.partial(queries_kernel, count=count, part=part,...  8.97 us
    pallas_call x1, Pallas kernels, project_keys(): pl.pallas_call(functools.partial(keys_kernel, count=count, part=part, fea...  7.88 us
  transfers between devices with their start and end apart: 33, of which 21 were waited for; matrix products, arithmetic and copies ran while one was open for 4% of the time, Pallas kernels for 12%

profile of v2, /device:TPU:513, one launch (start us, length us, event | category | flops | bytes accessed | tf_op | source)
XLA Modules:
  0.0 204.8 jit_solution(15753839834401572499)
XLA Ops:
  1.3 1.1 fusion.1
  2.4 12.5 %collective-permute-start.14 = (bf16[328,896]{1,0:T(8,128)(2,1)S(1)}, bf16[328,896]{1,0:T(8,128)(2,1)S(1)}, u32[]{:S(2)}, u32[]{:S(2)}) collective-permute-start(bf16[328,896]{1,0:T(8,128)(2,1)S(1)} %fusion.1), channel_id=1, source_target_pairs={{0,112},{8,120},{16,0},{24,8},{32,16},{40,24},{48,32},{56,40},{64,... | collective-permute-start | bytes 1763336 | tf_op jit(solution)/shard_map/ppermute | solution.py:31
  15.0 6.8 %collective-permute-done.14 = bf16[328,896]{1,0:T(8,128)(2,1)S(1)} collective-permute-done((bf16[328,896]{1,0:T(8,128)(2,1)S(1)}, bf16[328,896]{1,0:T(8,128)(2,1)S(1)}, u32[]{:S(2)}, u32[]{:S(2)}) %collective-permute-start.14) | collective-permute-done | bytes 587808 | tf_op jit(solution)/shard_map/ppermute | solution.py:31
  21.8 5.4 %collective-permute-start.16 = (bf16[328,896]{1,0:T(8,128)(2,1)S(1)}, bf16[328,896]{1,0:T(8,128)(2,1)S(1)}, u32[]{:S(2)}, u32[]{:S(2)}) collective-permute-start(bf16[328,896]{1,0:T(8,128)(2,1)S(1)} %collective-permute-done.14), channel_id=1, source_target_pairs={{0,112},{8,120},{16,0},{24,8},{32,16},{40,24},{48,32},{56,40},{64,... | collective-permute-start | bytes 1763336 | tf_op jit(solution)/shard_map/ppermute | solution.py:31
  27.2 2.0 bitcast_dynamic-update-slice_fusion.6
  29.1 0.9 bitcast_dynamic-update-slice_fusion.5
  30.0 6.3 %collective-permute-done.16 = bf16[328,896]{1,0:T(8,128)(2,1)S(1)} collective-permute-done((bf16[328,896]{1,0:T(8,128)(2,1)S(1)}, bf16[328,896]{1,0:T(8,128)(2,1)S(1)}, u32[]{:S(2)}, u32[]{:S(2)}) %collective-permute-start.16) | collective-permute-done | bytes 587808 | tf_op jit(solution)/shard_map/ppermute | solution.py:31
  36.3 3.1 %collective-permute-start.18 = (bf16[328,896]{1,0:T(8,128)(2,1)S(1)}, bf16[328,896]{1,0:T(8,128)(2,1)S(1)}, u32[]{:S(2)}, u32[]{:S(2)}) collective-permute-start(bf16[328,896]{1,0:T(8,128)(2,1)S(1)} %collective-permute-done.16), channel_id=1, source_target_pairs={{0,112},{8,120},{16,0},{24,8},{32,16},{40,24},{48,32},{56,40},{64,... | collective-permute-start | bytes 1763336 | tf_op jit(solution)/shard_map/ppermute | solution.py:31
  39.4 0.9 bitcast_dynamic-update-slice_fusion.4
  40.5 0.9 bitcast_dynamic-update-slice_fusion.3
  42.2 8.5 %collective-permute-done.18 = bf16[328,896]{1,0:T(8,128)(2,1)S(1)} collective-permute-done((bf16[328,896]{1,0:T(8,128)(2,1)S(1)}, bf16[328,896]{1,0:T(8,128)(2,1)S(1)}, u32[]{:S(2)}, u32[]{:S(2)}) %collective-permute-start.18) | collective-permute-done | bytes 587808 | tf_op jit(solution)/shard_map/ppermute | solution.py:31
  50.8 0.9 bitcast_dynamic-update-slice_fusion.1
  51.6 2.5 %collective-permute-done.19 = bf16[328,896]{1,0:T(8,128)(2,1)S(1)} collective-permute-done((bf16[328,896]{1,0:T(8,128)(2,1)S(1)}, bf16[328,896]{1,0:T(8,128)(2,1)S(1)}, u32[]{:S(2)}, u32[]{:S(2)}) %collective-permute-start.19) | collective-permute-done | bytes 587808 | tf_op jit(solution)/shard_map/ppermute | solution.py:30
  54.2 0.9 bitcast_dynamic-update-slice_fusion.refs_16_.mine
  55.1 10.9 %collective-permute-start.20 = (bf16[7,328,896]{2,1,0:T(8,128)(2,1)}, bf16[7,328,896]{2,1,0:T(8,128)(2,1)}, u32[]{:S(2)}, u32[]{:S(2)}) collective-permute-start(bf16[7,328,896]{2,1,0:T(8,128)(2,1)} %bitcast_dynamic-update-slice_fusion.refs_16_.mine), channel_id=1, source_target_pairs={{0,8},{8,0},{16,24},{24,16},{32,40},{40,32},{48,56},{56,48},{64,72... | collective-permute-start | bytes 12343304 | tf_op jit(solution)/shard_map/ppermute | solution.py:45
  66.2 2.6 %collective-permute-start.1 = (bf16[320,640]{1,0:T(8,128)(2,1)S(1)}, bf16[320,640]{1,0:T(8,128)(2,1)S(1)}, u32[]{:S(2)}, u32[]{:S(2)}) collective-permute-start(bf16[320,640]{1,0:T(8,128)(2,1)S(1)} %get-tuple-element.20.refs_0_), channel_id=1, source_target_pairs={{0,7},{1,0},{2,1},{3,2},{4,3},{5,4},{6,5},{7,6},{8,15},{9,8},{10,9... | collective-permute-start | bytes 1228808 | tf_op jit(solution)/shard_map/ppermute | solution.py:31
  68.9 1.4 collective-permute-start
  70.9 7.5 %collective-permute-done.4.refs_7_ = bf16[320,640]{1,0:T(8,128)(2,1)S(1)} collective-permute-done((bf16[320,640]{1,0:T(8,128)(2,1)S(1)}, bf16[320,640]{1,0:T(8,128)(2,1)S(1)}, u32[]{:S(2)}, u32[]{:S(2)}) %collective-permute-start.4) | collective-permute-done | bytes 409632 | tf_op jit(solution)/shard_map/ppermute | solution.py:30
  78.4 1.2 fusion.2
  79.9 7.3 %collective-permute-done.refs_15_ = bf16[320,640]{1,0:T(8,128)(2,1)S(1)} collective-permute-done((bf16[320,640]{1,0:T(8,128)(2,1)S(1)}, bf16[320,640]{1,0:T(8,128)(2,1)S(1)}, u32[]{:S(2)}, u32[]{:S(2)}) %collective-permute-start) | collective-permute-done | bytes 409632 | tf_op jit(solution)/shard_map/ppermute | solution.py:30
  87.2 2.3 %collective-permute-start.9 = (bf16[320,640]{1,0:T(8,128)(2,1)S(1)}, bf16[320,640]{1,0:T(8,128)(2,1)S(1)}, u32[]{:S(2)}, u32[]{:S(2)}) collective-permute-start(bf16[320,640]{1,0:T(8,128)(2,1)S(1)} %collective-permute-done.8.refs_9_), channel_id=1, source_target_pairs={{0,7},{1,0},{2,1},{3,2},{4,3},{5,4},{6,5},{7,6},{8,15},{9,8},{10,9... | collective-permute-start | bytes 1228808 | tf_op jit(solution)/shard_map/ppermute | solution.py:31
  89.6 6.4 %collective-permute-done.5.refs_6_ = bf16[320,640]{1,0:T(8,128)(2,1)S(1)} collective-permute-done((bf16[320,640]{1,0:T(8,128)(2,1)S(1)}, bf16[320,640]{1,0:T(8,128)(2,1)S(1)}, u32[]{:S(2)}, u32[]{:S(2)}) %collective-permute-start.5) | collective-permute-done | bytes 409632 | tf_op jit(solution)/shard_map/ppermute | solution.py:30
  95.9 0.9 collective-permute-done.2.refs_2_
  96.9 8.8 %collective-permute-done.9.refs_10_ = bf16[320,640]{1,0:T(8,128)(2,1)S(1)} collective-permute-done((bf16[320,640]{1,0:T(8,128)(2,1)S(1)}, bf16[320,640]{1,0:T(8,128)(2,1)S(1)}, u32[]{:S(2)}, u32[]{:S(2)}) %collective-permute-start.9) | collective-permute-done | bytes 409632 | tf_op jit(solution)/shard_map/ppermute | solution.py:31
  105.7 1.3 collective-permute-start.3
  106.9 3.7 %collective-permute-done.21.refs_18_.mine_mid = bf16[328,896]{1,0:T(8,128)(2,1)S(1)} collective-permute-done((bf16[328,896]{1,0:T(8,128)(2,1)S(1)}, bf16[328,896]{1,0:T(8,128)(2,1)S(1)}, u32[]{:S(2)}, u32[]{:S(2)}) %collective-permute-start.21) | collective-permute-done | bytes 587808 | tf_op jit(solution)/shard_map/ppermute | solution.py:37
  110.7 2.2 %collective-permute-start.22 = (bf16[328,896]{1,0:T(8,128)(2,1)S(1)}, bf16[328,896]{1,0:T(8,128)(2,1)S(1)}, u32[]{:S(2)}, u32[]{:S(2)}) collective-permute-start(bf16[328,896]{1,0:T(8,128)(2,1)S(1)} %collective-permute-done.21.refs_18_.mine_mid), channel_id=1, source_target_pairs={{0,8},{8,0},{16,24},{24,16},{32,40},{40,32},{48,56},{56,48},{64,72... | collective-permute-start | bytes 1763336 | tf_op jit(solution)/shard_map/ppermute | solution.py:45
  113.5 1.0 collective-permute-done.3.refs_3_
  114.5 8.8 %collective-permute-done.10.refs_11_ = bf16[320,640]{1,0:T(8,128)(2,1)S(1)} collective-permute-done((bf16[320,640]{1,0:T(8,128)(2,1)S(1)}, bf16[320,640]{1,0:T(8,128)(2,1)S(1)}, u32[]{:S(2)}, u32[]{:S(2)}) %collective-permute-start.10) | collective-permute-done | bytes 409632 | tf_op jit(solution)/shard_map/ppermute | solution.py:31
  123.3 2.5 %collective-permute-start.11 = (bf16[320,640]{1,0:T(8,128)(2,1)S(1)}, bf16[320,640]{1,0:T(8,128)(2,1)S(1)}, u32[]{:S(2)}, u32[]{:S(2)}) collective-permute-start(bf16[320,640]{1,0:T(8,128)(2,1)S(1)} %collective-permute-done.10.refs_11_), channel_id=1, source_target_pairs={{0,7},{1,0},{2,1},{3,2},{4,3},{5,4},{6,5},{7,6},{8,15},{9,8},{10,9... | collective-permute-start | bytes 1228808 | tf_op jit(solution)/shard_map/ppermute | solution.py:39
  125.8 7.9 %collective-permute-done.7.refs_4_ = bf16[320,640]{1,0:T(8,128)(2,1)S(1)} collective-permute-done((bf16[320,640]{1,0:T(8,128)(2,1)S(1)}, bf16[320,640]{1,0:T(8,128)(2,1)S(1)}, u32[]{:S(2)}, u32[]{:S(2)}) %collective-permute-start.7) | collective-permute-done | bytes 409632 | tf_op jit(solution)/shard_map/ppermute | solution.py:37
  133.7 7.9 %shard_map.95 = (bf16[640,256]{1,0:T(8,128)(2,1)S(1)}, s32[16,128]{1,0:T(8,128)S(1)}, bf16[640,5120]{1,0:T(8,128)(2,1)S(1)}) custom-call(s32[4]{0:T(128)S(1)} %pad_add_fusion.place, bf16[320,640]{1,0:T(8,128)(2,1)S(1)} %get-tuple-element.20.refs_0_, bf16[320,640]{1,0:T(8,128)(2,1)S(1)} %collective-permute-done.1.refs_1_, ...), custom_call_target="tpu_custom_call" | custom-call | flops 1677721600 | bytes 13107200 | tf_op jit(solution)/shard_map/pallas_call | solution.py:185
  141.7 1.4 collective-permute-start.23
  143.1 6.0 %collective-permute-done.25 = bf16[640,256]{1,0:T(8,128)(2,1)S(1)} collective-permute-done((bf16[640,256]{1,0:T(8,128)(2,1)S(1)}, bf16[640,256]{1,0:T(8,128)(2,1)S(1)}, u32[]{:S(2)}, u32[]{:S(2)}) %collective-permute-start.25) | collective-permute-done | bytes 327712 | tf_op jit(solution)/shard_map/ppermute | solution.py:31
  149.2 1.2 collective-permute-start.26
  150.8 5.0 %collective-permute-done.26 = bf16[640,256]{1,0:T(8,128)(2,1)S(1)} collective-permute-done((bf16[640,256]{1,0:T(8,128)(2,1)S(1)}, bf16[640,256]{1,0:T(8,128)(2,1)S(1)}, u32[]{:S(2)}, u32[]{:S(2)}) %collective-permute-start.26) | collective-permute-done | bytes 327712 | tf_op jit(solution)/shard_map/ppermute | solution.py:31
  155.8 2.5 %collective-permute-start.28 = (bf16[640,256]{1,0:T(8,128)(2,1)S(1)}, bf16[640,256]{1,0:T(8,128)(2,1)S(1)}, u32[]{:S(2)}, u32[]{:S(2)}) collective-permute-start(bf16[640,256]{1,0:T(8,128)(2,1)S(1)} %collective-permute-done.26), channel_id=1, source_target_pairs={{0,112},{8,120},{16,0},{24,8},{32,16},{40,24},{48,32},{56,40},{64,... | collective-permute-start | bytes 983048 | tf_op jit(solution)/shard_map/ppermute | solution.py:31
  158.7 3.6 %collective-permute-done.28 = bf16[640,256]{1,0:T(8,128)(2,1)S(1)} collective-permute-done((bf16[640,256]{1,0:T(8,128)(2,1)S(1)}, bf16[640,256]{1,0:T(8,128)(2,1)S(1)}, u32[]{:S(2)}, u32[]{:S(2)}) %collective-permute-start.28) | collective-permute-done | bytes 327712 | tf_op jit(solution)/shard_map/ppermute | solution.py:31
  162.3 3.4 %collective-permute-done.29 = bf16[640,256]{1,0:T(8,128)(2,1)S(1)} collective-permute-done((bf16[640,256]{1,0:T(8,128)(2,1)S(1)}, bf16[640,256]{1,0:T(8,128)(2,1)S(1)}, u32[]{:S(2)}, u32[]{:S(2)}) %collective-permute-start.29) | collective-permute-done | bytes 327712 | tf_op jit(solution)/shard_map/ppermute | solution.py:30
  165.8 4.8 %collective-permute-start.30 = (bf16[4480,256]{1,0:T(8,128)(2,1)S(1)}, bf16[4480,256]{1,0:T(8,128)(2,1)S(1)}, u32[]{:S(2)}, u32[]{:S(2)}) collective-permute-start(bf16[4480,256]{1,0:T(8,128)(2,1)S(1)} %constant_dynamic-update-slice_fusion.mine), channel_id=1, source_target_pairs={{0,8},{8,0},{16,24},{24,16},{32,40},{40,32},{48,56},{56,48},{64,72... | collective-permute-start | bytes 6881288 | tf_op jit(solution)/shard_map/ppermute | solution.py:45
  170.6 1.9 collective-permute-start.24
  172.6 9.0 %shard_map.96.q_in = bf16[5,640,128]{2,1,0:T(8,128)(2,1)S(1)} custom-call(s32[4]{0:T(128)S(1)} %pad_add_fusion.place, bf16[640,5120]{1,0:T(8,128)(2,1)S(1)} %get-tuple-element.17.x, bf16[7,328,896]{2,1,0:T(8,128)(2,1)} %bitcast_dynamic-update-slice_fusion.refs_16_.mine, bf16[7,328,896]{2,1,0:T(8,128)(2,1)} %collective-permute-done.20.refs_17_.other, ...), custom_call_target="tpu_custom_call" | custom-call | flops 4194304000 | bytes 6553600 | tf_op jit(solution)/shard_map/pallas_call | solution.py:223
  181.7 5.9 %shard_map.97.refs_0_ = bf16[640,640]{1,0:T(8,128)(2,1)} custom-call(s32[9]{0:T(128)S(1)} %pad_add_fusion.1.info, bf16[5,640,128]{2,1,0:T(8,128)(2,1)S(1)} %shard_map.96.q_in, bf16[640,256]{1,0:T(8,128)(2,1)S(1)} %collective-permute-done.23.far, bf16[640,256]{1,0:T(8,128)(2,1)S(1)} %collective-permute-done.24.near, bf16[640,256]{1,0:T(8,128)(2,1)S(1)} %get-tuple-element.18.own), custom_call_target="tpu_custom_call" | custom-call | flops 4000000000 | bytes 4000000 | tf_op jit(solution)/shard_map/pallas_call | solution.py:353
  187.6 2.8 %collective-permute-done.31.mine_mid = bf16[640,256]{1,0:T(8,128)(2,1)S(1)} collective-permute-done((bf16[640,256]{1,0:T(8,128)(2,1)S(1)}, bf16[640,256]{1,0:T(8,128)(2,1)S(1)}, u32[]{:S(2)}, u32[]{:S(2)}) %collective-permute-start.31) | collective-permute-done | bytes 327712 | tf_op jit(solution)/shard_map/ppermute | solution.py:39
  190.4 1.4 collective-permute-start.32
  191.8 6.9 %shard_map.98.refs_0_ = bf16[640,640]{1,0:T(8,128)(2,1)} custom-call(s32[9]{0:T(128)S(1)} %pad_add_fusion.1.info, bf16[5,640,128]{2,1,0:T(8,128)(2,1)S(1)} %shard_map.96.q_in, bf16[640,256]{1,0:T(8,128)(2,1)S(1)} %collective-permute-done.23.far, bf16[640,256]{1,0:T(8,128)(2,1)S(1)} %collective-permute-done.24.near, ...), custom_call_target="tpu_custom_call", output_to_operand_aliasing={{}: (5, {})} | custom-call | flops 4000000000 | bytes 4000000 | tf_op jit(solution)/shard_map/pallas_call | solution.py:353
  198.7 2.5 %shard_map.99 = bf16[640,640]{1,0:T(8,128)(2,1)} custom-call(s32[9]{0:T(128)S(1)} %pad_add_fusion.1.info, bf16[5,640,128]{2,1,0:T(8,128)(2,1)S(1)} %shard_map.96.q_in, bf16[640,256]{1,0:T(8,128)(2,1)S(1)} %collective-permute-done.23.far, bf16[640,256]{1,0:T(8,128)(2,1)S(1)} %collective-permute-done.24.near, ...), custom_call_target="tpu_custom_call", output_to_operand_aliasing={{}: (5, {})} | custom-call | flops 2000000000 | bytes 4000000 | tf_op jit(solution)/shard_map/pallas_call | solution.py:353
  201.3 3.3 %shard_map.100 = bf16[32,128,256]{2,1,0:T(8,128)(2,1)} custom-call(s32[4]{0:T(128)S(1)} %pad_add_fusion.place, s32[16,128]{1,0:T(8,128)S(1)} %get-tuple-element.19.labels, s32[1,32]{1,0:T(1,128)S(1)} %copy-done, bf16[4480,256]{1,0:T(8,128)(2,1)S(1)} %constant_dynamic-update-slice_fusion.mine, bf16[4480,256]{1,0:T(8,128)(2,1)S(1)} %collective-permute-done.30.other, ...), custom_call_target="tpu_custom_call" | custom-call | tf_op jit(solution)/shard_map/pallas_call | solution.py:437
  (60 shorter events, 4.7 us)
Async XLA Ops:
  2.4 19.3 %collective-permute-start.14 = (bf16[328,896]{1,0:T(8,128)(2,1)S(1)}, bf16[328,896]{1,0:T(8,128)(2,1)S(1)}, u32[]{:S(2)}, u32[]{:S(2)}) collective-permute-start(bf16[328,896]{1,0:T(8,128)(2,1)S(1)} %fusion.1), channel_id=1, source_target_pairs={{0,112},{8,120},{16,0},{24,8},{32,16},{40,24},{48,32},{56,40},{64,... | collective-permute-start | bytes 1763336 | tf_op jit(solution)/shard_map/ppermute | solution.py:31
  15.0 12.2 %collective-permute-start.15 = (bf16[328,896]{1,0:T(8,128)(2,1)S(1)}, bf16[328,896]{1,0:T(8,128)(2,1)S(1)}, u32[]{:S(2)}, u32[]{:S(2)}) collective-permute-start(bf16[328,896]{1,0:T(8,128)(2,1)S(1)} %fusion.1), channel_id=1, source_target_pairs={{0,16},{8,24},{16,32},{24,40},{32,48},{40,56},{48,64},{56,72},{64,... | collective-permute-start | bytes 1763336 | tf_op jit(solution)/shard_map/ppermute | solution.py:30
  21.8 14.5 %collective-permute-start.16 = (bf16[328,896]{1,0:T(8,128)(2,1)S(1)}, bf16[328,896]{1,0:T(8,128)(2,1)S(1)}, u32[]{:S(2)}, u32[]{:S(2)}) collective-permute-start(bf16[328,896]{1,0:T(8,128)(2,1)S(1)} %collective-permute-done.14), channel_id=1, source_target_pairs={{0,112},{8,120},{16,0},{24,8},{32,16},{40,24},{48,32},{56,40},{64,... | collective-permute-start | bytes 1763336 | tf_op jit(solution)/shard_map/ppermute | solution.py:31
  27.2 13.1 %collective-permute-start.17 = (bf16[328,896]{1,0:T(8,128)(2,1)S(1)}, bf16[328,896]{1,0:T(8,128)(2,1)S(1)}, u32[]{:S(2)}, u32[]{:S(2)}) collective-permute-start(bf16[328,896]{1,0:T(8,128)(2,1)S(1)} %collective-permute-done.15), channel_id=1, source_target_pairs={{0,16},{8,24},{16,32},{24,40},{32,48},{40,56},{48,64},{56,72},{64,... | collective-permute-start | bytes 1763336 | tf_op jit(solution)/shard_map/ppermute | solution.py:30
  36.3 14.5 %collective-permute-start.18 = (bf16[328,896]{1,0:T(8,128)(2,1)S(1)}, bf16[328,896]{1,0:T(8,128)(2,1)S(1)}, u32[]{:S(2)}, u32[]{:S(2)}) collective-permute-start(bf16[328,896]{1,0:T(8,128)(2,1)S(1)} %collective-permute-done.16), channel_id=1, source_target_pairs={{0,112},{8,120},{16,0},{24,8},{32,16},{40,24},{48,32},{56,40},{64,... | collective-permute-start | bytes 1763336 | tf_op jit(solution)/shard_map/ppermute | solution.py:31
  40.2 25.7 %copy-start.1 = (bf16[640,640]{1,0:T(8,128)(2,1)S(1)}, bf16[640,640]{1,0:T(8,128)(2,1)}, u32[]{:S(2)}) copy-start(bf16[640,640]{1,0:T(8,128)(2,1)} %param.8) | copy-start | bytes 2457604
  40.2 13.9 %collective-permute-start.19 = (bf16[328,896]{1,0:T(8,128)(2,1)S(1)}, bf16[328,896]{1,0:T(8,128)(2,1)S(1)}, u32[]{:S(2)}, u32[]{:S(2)}) collective-permute-start(bf16[328,896]{1,0:T(8,128)(2,1)S(1)} %collective-permute-done.17), channel_id=1, source_target_pairs={{0,16},{8,24},{16,32},{24,40},{32,48},{40,56},{48,64},{56,72},{64,... | collective-permute-start | bytes 1763336 | tf_op jit(solution)/shard_map/ppermute | solution.py:30
  42.2 28.1 %copy-start.3 = (s32[8]{0:T(128)S(1)}, s32[8]{0:T(128)}, u32[]{:S(2)}) copy-start(s32[8]{0:T(128)} %param.13) | copy-start | bytes 100
  42.2 28.3 %copy-start.2 = (bf16[5120]{0:T(1024)(128)(2,1)S(1)}, bf16[5120]{0:T(1024)(128)(2,1)}, u32[]{:S(2)}) copy-start(bf16[5120]{0:T(1024)(128)(2,1)} %param.9) | copy-start | bytes 30724
  55.1 78.6 %collective-permute-start.20 = (bf16[7,328,896]{2,1,0:T(8,128)(2,1)}, bf16[7,328,896]{2,1,0:T(8,128)(2,1)}, u32[]{:S(2)}, u32[]{:S(2)}) collective-permute-start(bf16[7,328,896]{2,1,0:T(8,128)(2,1)} %bitcast_dynamic-update-slice_fusion.refs_16_.mine), channel_id=1, source_target_pairs={{0,8},{8,0},{16,24},{24,16},{32,40},{40,32},{48,56},{56,48},{64,72... | collective-permute-start | bytes 12343304 | tf_op jit(solution)/shard_map/ppermute | solution.py:45
  66.0 12.3 %collective-permute-start.4 = (bf16[320,640]{1,0:T(8,128)(2,1)S(1)}, bf16[320,640]{1,0:T(8,128)(2,1)S(1)}, u32[]{:S(2)}, u32[]{:S(2)}) collective-permute-start(bf16[320,640]{1,0:T(8,128)(2,1)S(1)} %get-tuple-element.20.refs_0_), channel_id=1, source_target_pairs={{0,1},{1,2},{2,3},{3,4},{4,5},{5,6},{6,7},{7,0},{8,9},{9,10},{10,1... | collective-permute-start | bytes 1228808 | tf_op jit(solution)/shard_map/ppermute | solution.py:30
  66.2 21.0 %collective-permute-start.1 = (bf16[320,640]{1,0:T(8,128)(2,1)S(1)}, bf16[320,640]{1,0:T(8,128)(2,1)S(1)}, u32[]{:S(2)}, u32[]{:S(2)}) collective-permute-start(bf16[320,640]{1,0:T(8,128)(2,1)S(1)} %get-tuple-element.20.refs_0_), channel_id=1, source_target_pairs={{0,7},{1,0},{2,1},{3,2},{4,3},{5,4},{6,5},{7,6},{8,15},{9,8},{10,9... | collective-permute-start | bytes 1228808 | tf_op jit(solution)/shard_map/ppermute | solution.py:31
  68.8 18.4 %collective-permute-start.8 = (bf16[320,640]{1,0:T(8,128)(2,1)S(1)}, bf16[320,640]{1,0:T(8,128)(2,1)S(1)}, u32[]{:S(2)}, u32[]{:S(2)}) collective-permute-start(bf16[320,640]{1,0:T(8,128)(2,1)S(1)} %get-tuple-element.21.refs_8_), channel_id=1, source_target_pairs={{0,7},{1,0},{2,1},{3,2},{4,3},{5,4},{6,5},{7,6},{8,15},{9,8},{10,9... | collective-permute-start | bytes 1228808 | tf_op jit(solution)/shard_map/ppermute | solution.py:31
  68.9 18.3 %collective-permute-start = (bf16[320,640]{1,0:T(8,128)(2,1)S(1)}, bf16[320,640]{1,0:T(8,128)(2,1)S(1)}, u32[]{:S(2)}, u32[]{:S(2)}) collective-permute-start(bf16[320,640]{1,0:T(8,128)(2,1)S(1)} %get-tuple-element.21.refs_8_), channel_id=1, source_target_pairs={{0,1},{1,2},{2,3},{3,4},{4,5},{5,6},{6,7},{7,0},{8,9},{9,10},{10,1... | collective-permute-start | bytes 1228808 | tf_op jit(solution)/shard_map/ppermute | solution.py:30
  78.4 17.6 %collective-permute-start.5 = (bf16[320,640]{1,0:T(8,128)(2,1)S(1)}, bf16[320,640]{1,0:T(8,128)(2,1)S(1)}, u32[]{:S(2)}, u32[]{:S(2)}) collective-permute-start(bf16[320,640]{1,0:T(8,128)(2,1)S(1)} %collective-permute-done.4.refs_7_), channel_id=1, source_target_pairs={{0,1},{1,2},{2,3},{3,4},{4,5},{5,6},{6,7},{7,0},{8,9},{9,10},{10,1... | collective-permute-start | bytes 1228808 | tf_op jit(solution)/shard_map/ppermute | solution.py:30
  87.2 9.7 %collective-permute-start.2 = (bf16[320,640]{1,0:T(8,128)(2,1)S(1)}, bf16[320,640]{1,0:T(8,128)(2,1)S(1)}, u32[]{:S(2)}, u32[]{:S(2)}) collective-permute-start(bf16[320,640]{1,0:T(8,128)(2,1)S(1)} %collective-permute-done.1.refs_1_), channel_id=1, source_target_pairs={{0,7},{1,0},{2,1},{3,2},{4,3},{5,4},{6,5},{7,6},{8,15},{9,8},{10,9... | collective-permute-start | bytes 1228808 | tf_op jit(solution)/shard_map/ppermute | solution.py:31
  87.2 18.4 %collective-permute-start.9 = (bf16[320,640]{1,0:T(8,128)(2,1)S(1)}, bf16[320,640]{1,0:T(8,128)(2,1)S(1)}, u32[]{:S(2)}, u32[]{:S(2)}) collective-permute-start(bf16[320,640]{1,0:T(8,128)(2,1)S(1)} %collective-permute-done.8.refs_9_), channel_id=1, source_target_pairs={{0,7},{1,0},{2,1},{3,2},{4,3},{5,4},{6,5},{7,6},{8,15},{9,8},{10,9... | collective-permute-start | bytes 1228808 | tf_op jit(solution)/shard_map/ppermute | solution.py:31
  89.6 17.4 %collective-permute-start.12 = (bf16[320,640]{1,0:T(8,128)(2,1)S(1)}, bf16[320,640]{1,0:T(8,128)(2,1)S(1)}, u32[]{:S(2)}, u32[]{:S(2)}) collective-permute-start(bf16[320,640]{1,0:T(8,128)(2,1)S(1)} %collective-permute-done.refs_15_), channel_id=1, source_target_pairs={{0,1},{1,2},{2,3},{3,4},{4,5},{5,6},{6,7},{7,0},{8,9},{9,10},{10,1... | collective-permute-start | bytes 1228808 | tf_op jit(solution)/shard_map/ppermute | solution.py:30
  95.9 14.7 %collective-permute-start.21 = (bf16[328,896]{1,0:T(8,128)(2,1)S(1)}, bf16[328,896]{1,0:T(8,128)(2,1)S(1)}, u32[]{:S(2)}, u32[]{:S(2)}) collective-permute-start(bf16[328,896]{1,0:T(8,128)(2,1)S(1)} %collective-permute-done.19), channel_id=1, source_target_pairs={{0,16},{8,24},{16,32},{24,40},{32,48},{40,56},{48,64},{56,72},{64,... | collective-permute-start | bytes 1763336 | tf_op jit(solution)/shard_map/ppermute | solution.py:37
  96.9 16.6 %collective-permute-start.6 = (bf16[320,640]{1,0:T(8,128)(2,1)S(1)}, bf16[320,640]{1,0:T(8,128)(2,1)S(1)}, u32[]{:S(2)}, u32[]{:S(2)}) collective-permute-start(bf16[320,640]{1,0:T(8,128)(2,1)S(1)} %collective-permute-done.5.refs_6_), channel_id=1, source_target_pairs={{0,1},{1,2},{2,3},{3,4},{4,5},{5,6},{6,7},{7,0},{8,9},{9,10},{10,1... | collective-permute-start | bytes 1228808 | tf_op jit(solution)/shard_map/ppermute | solution.py:30
  105.7 8.8 %collective-permute-start.3 = (bf16[320,640]{1,0:T(8,128)(2,1)S(1)}, bf16[320,640]{1,0:T(8,128)(2,1)S(1)}, u32[]{:S(2)}, u32[]{:S(2)}) collective-permute-start(bf16[320,640]{1,0:T(8,128)(2,1)S(1)} %collective-permute-done.2.refs_2_), channel_id=1, source_target_pairs={{0,7},{1,0},{2,1},{3,2},{4,3},{5,4},{6,5},{7,6},{8,15},{9,8},{10,9... | collective-permute-start | bytes 1228808 | tf_op jit(solution)/shard_map/ppermute | solution.py:31
  106.9 16.3 %collective-permute-start.10 = (bf16[320,640]{1,0:T(8,128)(2,1)S(1)}, bf16[320,640]{1,0:T(8,128)(2,1)S(1)}, u32[]{:S(2)}, u32[]{:S(2)}) collective-permute-start(bf16[320,640]{1,0:T(8,128)(2,1)S(1)} %collective-permute-done.9.refs_10_), channel_id=1, source_target_pairs={{0,7},{1,0},{2,1},{3,2},{4,3},{5,4},{6,5},{7,6},{8,15},{9,8},{10,9... | collective-permute-start | bytes 1228808 | tf_op jit(solution)/shard_map/ppermute | solution.py:31
  110.7 23.0 %collective-permute-start.22 = (bf16[328,896]{1,0:T(8,128)(2,1)S(1)}, bf16[328,896]{1,0:T(8,128)(2,1)S(1)}, u32[]{:S(2)}, u32[]{:S(2)}) collective-permute-start(bf16[328,896]{1,0:T(8,128)(2,1)S(1)} %collective-permute-done.21.refs_18_.mine_mid), channel_id=1, source_target_pairs={{0,8},{8,0},{16,24},{24,16},{32,40},{40,32},{48,56},{56,48},{64,72... | collective-permute-start | bytes 1763336 | tf_op jit(solution)/shard_map/ppermute | solution.py:45
  113.5 12.3 %collective-permute-start.13 = (bf16[320,640]{1,0:T(8,128)(2,1)S(1)}, bf16[320,640]{1,0:T(8,128)(2,1)S(1)}, u32[]{:S(2)}, u32[]{:S(2)}) collective-permute-start(bf16[320,640]{1,0:T(8,128)(2,1)S(1)} %collective-permute-done.12.refs_14_), channel_id=1, source_target_pairs={{0,1},{1,2},{2,3},{3,4},{4,5},{5,6},{6,7},{7,0},{8,9},{9,10},{10,1... | collective-permute-start | bytes 1228808 | tf_op jit(solution)/shard_map/ppermute | solution.py:30
  114.5 19.2 %collective-permute-start.7 = (bf16[320,640]{1,0:T(8,128)(2,1)S(1)}, bf16[320,640]{1,0:T(8,128)(2,1)S(1)}, u32[]{:S(2)}, u32[]{:S(2)}) collective-permute-start(bf16[320,640]{1,0:T(8,128)(2,1)S(1)} %collective-permute-done.6.refs_5_), channel_id=1, source_target_pairs={{0,1},{1,2},{2,3},{3,4},{4,5},{5,6},{6,7},{7,0},{8,9},{9,10},{10,1... | collective-permute-start | bytes 1228808 | tf_op jit(solution)/shard_map/ppermute | solution.py:37
  123.3 10.4 %collective-permute-start.11 = (bf16[320,640]{1,0:T(8,128)(2,1)S(1)}, bf16[320,640]{1,0:T(8,128)(2,1)S(1)}, u32[]{:S(2)}, u32[]{:S(2)}) collective-permute-start(bf16[320,640]{1,0:T(8,128)(2,1)S(1)} %collective-permute-done.10.refs_11_), channel_id=1, source_target_pairs={{0,7},{1,0},{2,1},{3,2},{4,3},{5,4},{6,5},{7,6},{8,15},{9,8},{10,9... | collective-permute-start | bytes 1228808 | tf_op jit(solution)/shard_map/ppermute | solution.py:39
  141.6 7.6 %collective-permute-start.25 = (bf16[640,256]{1,0:T(8,128)(2,1)S(1)}, bf16[640,256]{1,0:T(8,128)(2,1)S(1)}, u32[]{:S(2)}, u32[]{:S(2)}) collective-permute-start(bf16[640,256]{1,0:T(8,128)(2,1)S(1)} %get-tuple-element.18.own), channel_id=1, source_target_pairs={{0,112},{8,120},{16,0},{24,8},{32,16},{40,24},{48,32},{56,40},{64,... | collective-permute-start | bytes 983048 | tf_op jit(solution)/shard_map/ppermute | solution.py:31
  141.7 9.0 %collective-permute-start.23 = (bf16[640,256]{1,0:T(8,128)(2,1)S(1)}, bf16[640,256]{1,0:T(8,128)(2,1)S(1)}, u32[]{:S(2)}, u32[]{:S(2)}) collective-permute-start(bf16[640,256]{1,0:T(8,128)(2,1)S(1)} %get-tuple-element.18.own), channel_id=1, source_target_pairs={{0,16},{8,24},{16,32},{24,40},{32,48},{40,56},{48,64},{56,72},{64,... | collective-permute-start | bytes 983048 | tf_op jit(solution)/shard_map/ppermute | solution.py:30
  149.2 6.6 %collective-permute-start.26 = (bf16[640,256]{1,0:T(8,128)(2,1)S(1)}, bf16[640,256]{1,0:T(8,128)(2,1)S(1)}, u32[]{:S(2)}, u32[]{:S(2)}) collective-permute-start(bf16[640,256]{1,0:T(8,128)(2,1)S(1)} %collective-permute-done.25), channel_id=1, source_target_pairs={{0,112},{8,120},{16,0},{24,8},{32,16},{40,24},{48,32},{56,40},{64,... | collective-permute-start | bytes 983048 | tf_op jit(solution)/shard_map/ppermute | solution.py:31
  150.7 7.9 %collective-permute-start.27 = (bf16[640,256]{1,0:T(8,128)(2,1)S(1)}, bf16[640,256]{1,0:T(8,128)(2,1)S(1)}, u32[]{:S(2)}, u32[]{:S(2)}) collective-permute-start(bf16[640,256]{1,0:T(8,128)(2,1)S(1)} %collective-permute-done.23.far), channel_id=1, source_target_pairs={{0,16},{8,24},{16,32},{24,40},{32,48},{40,56},{48,64},{56,72},{64,... | collective-permute-start | bytes 983048 | tf_op jit(solution)/shard_map/ppermute | solution.py:30
  155.8 6.5 %collective-permute-start.28 = (bf16[640,256]{1,0:T(8,128)(2,1)S(1)}, bf16[640,256]{1,0:T(8,128)(2,1)S(1)}, u32[]{:S(2)}, u32[]{:S(2)}) collective-permute-start(bf16[640,256]{1,0:T(8,128)(2,1)S(1)} %collective-permute-done.26), channel_id=1, source_target_pairs={{0,112},{8,120},{16,0},{24,8},{32,16},{40,24},{48,32},{56,40},{64,... | collective-permute-start | bytes 983048 | tf_op jit(solution)/shard_map/ppermute | solution.py:31
  158.6 7.1 %collective-permute-start.29 = (bf16[640,256]{1,0:T(8,128)(2,1)S(1)}, bf16[640,256]{1,0:T(8,128)(2,1)S(1)}, u32[]{:S(2)}, u32[]{:S(2)}) collective-permute-start(bf16[640,256]{1,0:T(8,128)(2,1)S(1)} %collective-permute-done.27), channel_id=1, source_target_pairs={{0,16},{8,24},{16,32},{24,40},{32,48},{40,56},{48,64},{56,72},{64,... | collective-permute-start | bytes 983048 | tf_op jit(solution)/shard_map/ppermute | solution.py:30
  165.8 35.5 %collective-permute-start.30 = (bf16[4480,256]{1,0:T(8,128)(2,1)S(1)}, bf16[4480,256]{1,0:T(8,128)(2,1)S(1)}, u32[]{:S(2)}, u32[]{:S(2)}) collective-permute-start(bf16[4480,256]{1,0:T(8,128)(2,1)S(1)} %constant_dynamic-update-slice_fusion.mine), channel_id=1, source_target_pairs={{0,8},{8,0},{16,24},{24,16},{32,40},{40,32},{48,56},{56,48},{64,72... | collective-permute-start | bytes 6881288 | tf_op jit(solution)/shard_map/ppermute | solution.py:45
  170.6 11.1 %collective-permute-start.24 = (bf16[640,256]{1,0:T(8,128)(2,1)S(1)}, bf16[640,256]{1,0:T(8,128)(2,1)S(1)}, u32[]{:S(2)}, u32[]{:S(2)}) collective-permute-start(bf16[640,256]{1,0:T(8,128)(2,1)S(1)} %get-tuple-element.18.own), channel_id=1, source_target_pairs={{0,8},{8,16},{16,24},{24,32},{32,40},{40,48},{48,56},{56,64},{64,7... | collective-permute-start | bytes 983048 | tf_op jit(solution)/shard_map/ppermute | solution.py:497
  181.5 8.9 %collective-permute-start.31 = (bf16[640,256]{1,0:T(8,128)(2,1)S(1)}, bf16[640,256]{1,0:T(8,128)(2,1)S(1)}, u32[]{:S(2)}, u32[]{:S(2)}) collective-permute-start(bf16[640,256]{1,0:T(8,128)(2,1)S(1)} %collective-permute-done.28), channel_id=1, source_target_pairs={{0,112},{8,120},{16,0},{24,8},{32,16},{40,24},{48,32},{56,40},{64,... | collective-permute-start | bytes 983048 | tf_op jit(solution)/shard_map/ppermute | solution.py:39
  190.4 10.9 %collective-permute-start.32 = (bf16[640,256]{1,0:T(8,128)(2,1)S(1)}, bf16[640,256]{1,0:T(8,128)(2,1)S(1)}, u32[]{:S(2)}, u32[]{:S(2)}) collective-permute-start(bf16[640,256]{1,0:T(8,128)(2,1)S(1)} %collective-permute-done.31.mine_mid), channel_id=1, source_target_pairs={{0,8},{8,0},{16,24},{24,16},{32,40},{40,32},{48,56},{56,48},{64,72... | collective-permute-start | bytes 983048 | tf_op jit(solution)/shard_map/ppermute | solution.py:45
  198.7 2.6 %copy-start = (s32[1,32]{1,0:T(1,128)S(1)}, s32[1,32]{1,0:T(1,128)}, u32[]{:S(2)}) copy-start(s32[1,32]{1,0:T(1,128)} %table.1) | copy-start | bytes 388
